TPU v7x, 128 devices: a whole 4x4x4 slice. The times are simulated.
128 devices in a mesh: row: 2 (over core), col: 64 (over z, y, x).
Axes of the slice: x: 4, y: 4, z: 4, core: 2. Of those that a mesh axis runs over, the one named last changes fastest.
Arguments:
- v_panels: float32 [6144, 6144], P('row', 'col')
- t_factors: float32 [192, 32, 32], P('col')
- z_vectors: float32 [6144, 4096], P(None, ('col', 'row'))
Outputs:
- output: float32 [6144, 4096], P('row', 'col')
All inputs are finite; a program needn't handle non-finite values.
Results may differ from a plain program's by a relative error of at most 0.001.
Values sent between devices are 32-bit elements.
A program may use at most 1 GiB of HBM per device.

v0:
```python
import jax
import jax.numpy as jnp
from jax import lax
from jax.sharding import PartitionSpec as P, NamedSharding

HIGHEST = lax.Precision.HIGHEST


def solution(mesh):
    col_devs = mesh.shape['col']

    def local_apply(v_loc, t_loc, z_loc):
        panel_width = t_loc.shape[1]
        groups = t_loc.shape[0]
        x_loc = lax.all_to_all(z_loc, 'row', 0, 1, tiled=True)

        def group_step(step_idx, x_cur):
            group_idx = groups - 1 - step_idx
            v_blk = lax.dynamic_slice_in_dim(v_loc, group_idx * panel_width, panel_width, axis=1)
            t_blk = lax.dynamic_index_in_dim(t_loc, group_idx, axis=0, keepdims=False)
            v_group = lax.all_gather(v_blk, 'col', axis=0)
            t_group = lax.all_gather(t_blk, 'col', axis=0)

            def panel_step(pos_idx, x_in):
                col_pos = col_devs - 1 - pos_idx
                v_j = lax.dynamic_index_in_dim(v_group, col_pos, axis=0, keepdims=False)
                t_j = lax.dynamic_index_in_dim(t_group, col_pos, axis=0, keepdims=False)
                w_part = jnp.einsum('na,nk->ak', v_j, x_in, precision=HIGHEST, preferred_element_type=jnp.float32)
                w_full = lax.psum(w_part, 'row')
                y_mat = jnp.dot(t_j, w_full, precision=HIGHEST, preferred_element_type=jnp.float32)
                return x_in - jnp.dot(v_j, y_mat, precision=HIGHEST, preferred_element_type=jnp.float32)

            return lax.fori_loop(0, col_devs, panel_step, x_cur)

        return lax.fori_loop(0, groups, group_step, x_loc)

    return jax.shard_map(local_apply, mesh=mesh,
                         in_specs=(P('row', 'col'), P('col', None, None), P(None, ('col', 'row'))),
                         out_specs=P('row', 'col'), check_vma=False)
```

profile of v0, /device:TPU:1, one launch (start us, length us, event | category | flops | bytes accessed | tf_op | source)
XLA Modules:
  0.0 3364.8 jit_solution(15263398911110827549)
XLA Ops:
  8.6 4.9 all-to-all-start
  14.8 3342.6 %while.44 = (s32[]{:T(128)}, f32[3072,64]{0,1:T(8,128)S(1)}, f32[3072,96]{0,1:T(8,128)}, f32[3,32,32]{2,1,0:T(8,128)}, s32[]{:T(128)}, /*index=5*/s32[]{:T(128)}...) while((s32[]{:T(128)}, f32[3072,64]{0,1:T(8,128)S(1)}, ...), condition=%wide.region_4.5_spmd, body=%wide.region_0.4_spmd.sunk | while | flops 151980048 | bytes 160780800 | solution.py:35
  18.2 165.4 %all_gather.32 = f32[64,32,32]{2,1,0:T(8,128)S(1)} all-gather(f32[1,32,32]{2,1,0:T(8,128)S(1)} %constant_dynamic-slice_fusion.5), channel_id=1, replica_groups=mesh['row'=2,'col'=64] {'col'}, dimensions={0}, use_global_device_ids=true | all-gather | bytes 266240 | tf_op jit(solution)/shard_map/while/body/eval_jaxpr/all_gather | solution.py:22
  183.6 239.7 %all-gather.5.cloned.1.call-done = f32[196608,32]{1,0:T(8,128)} async-done(((f32[3072,32]{1,0:T(8,128)}), f32[196608,32]{1,0:T(8,128)}) %all-gather.5.cloned.1.call-update) | async-done | bytes 25165840 | tf_op jit(solution)/shard_map/while/body/eval_jaxpr/all_gather | solution.py:21
  423.3 708.7 %while.45 = (s32[]{:T(128)}, f32[3072,64]{0,1:T(8,128)S(1)}, f32[64,3072,32]{2,1,0:T(8,128)}, f32[64,32,32]{2,1,0:T(8,128)S(1)}, s32[]{:T(128)}, /*index=5*/s32[]{:T(128)}, s32[]{:T(128)}, s32[]{:T(128)}) while((s32[]{:T(128)}, f32[3072,64]{0,1:T(8,128)S(1)}, f32[64,3072,32]{2,1,0:T(8,128)}, f32[64,32,32]{2,1,0:T(8,128)S(1)}, s32[]{:T(128)}, ...), condition=%wide.region_3.3_spmd, body=%wide.region_1.2_spmd.sunk | while | flops 151980032 | bytes 5578895 | solution.py:33
  427.3 4.1 psum.14
  435.1 4.0 fusion.28
  457.2 4.0 fusion.28
  468.2 4.0 fusion.28
  501.5 4.0 fusion.28
  523.6 4.0 fusion.28
  534.6 4.0 fusion.28
  590.0 4.0 fusion.28
  601.0 4.0 fusion.28
  623.1 4.0 fusion.28
  656.4 4.0 fusion.28
  667.4 4.0 fusion.28
  689.5 4.0 fusion.28
  722.8 4.0 fusion.28
  733.7 4.0 fusion.28
  744.9 4.0 fusion.28
  755.9 4.0 fusion.28
  789.2 4.0 fusion.28
  800.1 4.0 fusion.28
  811.3 4.0 fusion.28
  822.3 4.0 fusion.28
  855.6 4.0 fusion.28
  877.7 4.0 fusion.28
  888.7 4.0 fusion.28
  921.9 4.0 fusion.28
  944.1 4.0 fusion.28
  955.1 4.0 fusion.28
  1010.5 4.0 fusion.28
  1021.4 4.0 fusion.28
  1043.6 4.0 fusion.28
  1076.9 4.0 fusion.28
  1087.8 4.0 fusion.28
  1110.0 4.0 fusion.28
  1135.6 160.9 %all_gather.32 = f32[64,32,32]{2,1,0:T(8,128)S(1)} all-gather(f32[1,32,32]{2,1,0:T(8,128)S(1)} %constant_dynamic-slice_fusion.5), channel_id=1, replica_groups=mesh['row'=2,'col'=64] {'col'}, dimensions={0}, use_global_device_ids=true | all-gather | bytes 266240 | tf_op jit(solution)/shard_map/while/body/eval_jaxpr/all_gather | solution.py:22
  1296.4 239.6 %all-gather.5.cloned.1.call-done = f32[196608,32]{1,0:T(8,128)} async-done(((f32[3072,32]{1,0:T(8,128)}), f32[196608,32]{1,0:T(8,128)}) %all-gather.5.cloned.1.call-update) | async-done | bytes 25165840 | tf_op jit(solution)/shard_map/while/body/eval_jaxpr/all_gather | solution.py:21
  1536.0 708.7 %while.45 = (s32[]{:T(128)}, f32[3072,64]{0,1:T(8,128)S(1)}, f32[64,3072,32]{2,1,0:T(8,128)}, f32[64,32,32]{2,1,0:T(8,128)S(1)}, s32[]{:T(128)}, /*index=5*/s32[]{:T(128)}, s32[]{:T(128)}, s32[]{:T(128)}) while((s32[]{:T(128)}, f32[3072,64]{0,1:T(8,128)S(1)}, f32[64,3072,32]{2,1,0:T(8,128)}, f32[64,32,32]{2,1,0:T(8,128)S(1)}, s32[]{:T(128)}, ...), condition=%wide.region_3.3_spmd, body=%wide.region_1.2_spmd.sunk | while | flops 151980032 | bytes 5578895 | solution.py:33
  1540.0 4.1 psum.14
  1580.9 4.0 fusion.28
  1614.1 4.0 fusion.28
  1647.3 4.0 fusion.28
  1669.4 4.0 fusion.28
  1680.5 4.0 fusion.28
  1702.7 4.0 fusion.28
  1713.6 4.0 fusion.28
  1735.8 4.0 fusion.28
  1746.9 4.0 fusion.28
  1769.1 4.0 fusion.28
  1780.0 4.0 fusion.28
  1802.2 4.0 fusion.28
  1813.3 4.0 fusion.28
  1835.4 4.0 fusion.28
  1846.4 4.0 fusion.28
  1868.6 4.0 fusion.28
  1879.7 4.0 fusion.28
  1901.8 4.0 fusion.28
  2248.2 160.8 %all_gather.32 = f32[64,32,32]{2,1,0:T(8,128)S(1)} all-gather(f32[1,32,32]{2,1,0:T(8,128)S(1)} %constant_dynamic-slice_fusion.5), channel_id=1, replica_groups=mesh['row'=2,'col'=64] {'col'}, dimensions={0}, use_global_device_ids=true | all-gather | bytes 266240 | tf_op jit(solution)/shard_map/while/body/eval_jaxpr/all_gather | solution.py:22
  2409.1 239.6 %all-gather.5.cloned.1.call-done = f32[196608,32]{1,0:T(8,128)} async-done(((f32[3072,32]{1,0:T(8,128)}), f32[196608,32]{1,0:T(8,128)}) %all-gather.5.cloned.1.call-update) | async-done | bytes 25165840 | tf_op jit(solution)/shard_map/while/body/eval_jaxpr/all_gather | solution.py:21
  2648.7 708.7 %while.45 = (s32[]{:T(128)}, f32[3072,64]{0,1:T(8,128)S(1)}, f32[64,3072,32]{2,1,0:T(8,128)}, f32[64,32,32]{2,1,0:T(8,128)S(1)}, s32[]{:T(128)}, /*index=5*/s32[]{:T(128)}, s32[]{:T(128)}, s32[]{:T(128)}) while((s32[]{:T(128)}, f32[3072,64]{0,1:T(8,128)S(1)}, f32[64,3072,32]{2,1,0:T(8,128)}, f32[64,32,32]{2,1,0:T(8,128)S(1)}, s32[]{:T(128)}, ...), condition=%wide.region_3.3_spmd, body=%wide.region_1.2_spmd.sunk | while | flops 151980032 | bytes 5578895 | solution.py:33
  2652.7 4.1 psum.14
  (733 shorter events, 1923.4 us)
Async XLA Ops:
  8.6 6.2 all-to-all-start
  14.8 408.5 %all-gather.5.cloned.1.call-start = ((), (), s32[]{:S(2)}) async-start(), calls=%async_computation.1 | async-start | bytes 102236160 | tf_op jit(solution)/shard_map/while/body/eval_jaxpr/all_gather | solution.py:21
  1132.1 403.9 %all-gather.5.cloned.1.call-start = ((), (), s32[]{:S(2)}) async-start(), calls=%async_computation.1 | async-start | bytes 102236160 | tf_op jit(solution)/shard_map/while/body/eval_jaxpr/all_gather | solution.py:21
  2244.8 403.9 %all-gather.5.cloned.1.call-start = ((), (), s32[]{:S(2)}) async-start(), calls=%async_computation.1 | async-start | bytes 102236160 | tf_op jit(solution)/shard_map/while/body/eval_jaxpr/all_gather | solution.py:21
Sparse Core Ops, SparseCore 0:
  18.4 404.9 all-gather.4
  1135.7 400.3 all-gather.4
  2248.3 400.2 all-gather.4
where the time goes:
time: 3380 us; the launch traced here: 3360 us
  matrix products  1460 us (43%)
  blocking collectives  1150 us (34%)
  waiting for transfers between devices  720 us (21%)
    dot_general x192, matrix products, panel_step(): jnp.einsum('na,nk->ak', v_j, x_in, precision=HIGHEST, preferred_element_t...  765 us
    all_gather x3, waiting for transfers between devices, group_step(): v_group = lax.all_gather(v_blk, 'col', axis=0)  719 us
    dot_general x192, matrix products, panel_step(): jnp.dot(v_j, y_mat, precision=HIGHEST, preferred_element_type=jnp.float32)  666 us
    psum x192, blocking collectives, panel_step(): w_full = lax.psum(w_part, 'row')  664 us
    all_gather x3, blocking collectives, group_step(): t_group = lax.all_gather(t_blk, 'col', axis=0)  487 us
  transfers between devices with their start and end apart: 4, of which 4 were waited for; matrix products, arithmetic and copies ran while one was open for 0% of the time, Pallas kernels for 0%

commit v1 on v0

v1 whole, which is shorter than its diff:
```python
import functools

import jax
import jax.numpy as jnp
from jax import lax
from jax.experimental import pallas as pl
from jax.experimental.pallas import tpu as pltpu
from jax.sharding import PartitionSpec as P

HIGHEST = lax.Precision.HIGHEST
BLOCK = 256
CHUNK = 512


def dot_nn(a, b):
    return lax.dot_general(a, b, (((1,), (0,)), ((), ())), precision=HIGHEST, preferred_element_type=jnp.float32)


def dot_nt(a, b):
    return lax.dot_general(a, b, (((1,), (1,)), ((), ())), precision=HIGHEST, preferred_element_type=jnp.float32)


def group_kernel(dims, vt_hbm, xin_ref, out_ref, vbuf, part, other, v_sem, send_sem, recv_sem):
    blocks, rows, first_row, step_rows, width, chunk = dims
    cols = xin_ref.shape[0]
    mate = 1 - lax.axis_index('row')

    barrier = pltpu.get_barrier_semaphore()
    pl.semaphore_signal(barrier, inc=1, device_id={'row': mate}, device_id_type=pl.DeviceIdType.MESH)
    pl.semaphore_wait(barrier, 1)

    def fetch(blk, slot):
        src = vt_hbm.at[pl.ds(pl.multiple_of(blk * BLOCK, BLOCK), BLOCK), :]
        return pltpu.make_async_copy(src, vbuf.at[slot], v_sem.at[slot])

    fetch(blocks - 1, 0).start()
    out_ref[...] = xin_ref[...]

    row_id = lax.broadcasted_iota(jnp.int32, (BLOCK, BLOCK), 0)
    col_id = lax.broadcasted_iota(jnp.int32, (BLOCK, BLOCK), 1)

    def block_step(step, carry):
        blk = blocks - 1 - step
        slot = lax.rem(step, 2)
        fetch(blk, slot).wait()

        @pl.when(step + 1 < blocks)
        def _():
            fetch(blk - 1, 1 - slot).start()

        start = (blk * step_rows) // chunk
        part[slot] = jnp.zeros(part.shape[1:], jnp.float32)

        def gather_products(c, carry):
            at = pl.multiple_of(c * chunk, chunk)
            v_c = vbuf[slot, :, pl.ds(at, chunk)]
            x_c = out_ref[:, pl.ds(first_row + at, chunk)]
            part[slot] += dot_nt(jnp.concatenate([x_c, v_c], axis=0), v_c)
            return carry

        lax.fori_loop(start, rows // chunk, gather_products, 0)

        swap = pltpu.make_async_remote_copy(
            src_ref=part.at[slot], dst_ref=other.at[slot], send_sem=send_sem.at[slot], recv_sem=recv_sem.at[slot],
            device_id={'row': mate}, device_id_type=pl.DeviceIdType.MESH)
        swap.start()
        swap.wait()

        w_t = part[slot, :cols] + other[slot, :cols]
        gram = part[slot, cols:] + other[slot, cols:]
        t_rows = vbuf[slot, :, rows:rows + 128]
        t_mat = jnp.concatenate([t_rows, t_rows], axis=1)
        t_mat = jnp.where(row_id // width == col_id // width, t_mat, 0.0)
        size = width
        while size < BLOCK:
            pick = (row_id // size + 1 == col_id // size) & (row_id // (2 * size) == col_id // (2 * size))
            t_mat = t_mat - dot_nn(dot_nn(t_mat, jnp.where(pick, gram, 0.0)), t_mat)
            size *= 2
        y_t = dot_nt(w_t, t_mat)

        def update(c, carry):
            at = pl.multiple_of(c * chunk, chunk)
            out_ref[:, pl.ds(first_row + at, chunk)] -= dot_nn(y_t, vbuf[slot, :, pl.ds(at, chunk)])
            return carry

        lax.fori_loop(start, rows // chunk, update, 0)
        return carry

    lax.fori_loop(0, blocks, block_step, 0)


def apply_group(x_t, vt, group, width, row_devs):
    cols, local_rows = x_t.shape
    group_cols, padded = vt.shape
    rows = padded - 128
    chunk = next(size for size in (CHUNK, 256, 128) if rows % size == 0)
    blocks = group_cols // BLOCK
    dims = (blocks, rows, local_rows - rows, BLOCK // row_devs, width, chunk)
    flops = 12 * blocks * rows * BLOCK * (BLOCK + 2 * cols)
    return pl.pallas_call(
        functools.partial(group_kernel, dims),
        out_shape=jax.ShapeDtypeStruct(x_t.shape, jnp.float32),
        in_specs=[pl.BlockSpec(memory_space=pl.ANY), pl.BlockSpec(memory_space=pltpu.VMEM)],
        out_specs=pl.BlockSpec(memory_space=pltpu.VMEM),
        scratch_shapes=[
            pltpu.VMEM((2, BLOCK, padded), jnp.float32),
            pltpu.VMEM((2, cols + BLOCK, BLOCK), jnp.float32),
            pltpu.VMEM((2, cols + BLOCK, BLOCK), jnp.float32),
            pltpu.SemaphoreType.DMA((2,)),
            pltpu.SemaphoreType.DMA((2,)),
            pltpu.SemaphoreType.DMA((2,)),
        ],
        cost_estimate=pl.CostEstimate(flops=flops, bytes_accessed=4 * group_cols * padded, transcendentals=0),
        compiler_params=pltpu.CompilerParams(collective_id=group, has_side_effects=True,
                                             vmem_limit_bytes=40 * 1024 * 1024),
    )(vt, x_t)


def solution(mesh):
    row_devs = mesh.shape['row']
    col_devs = mesh.shape['col']

    def local_apply(v_loc, t_loc, z_loc):
        groups, width = t_loc.shape[0], t_loc.shape[1]
        local_rows = v_loc.shape[0]
        gathered = {}
        for group in reversed(range(groups)):
            first_row = group * col_devs * width // row_devs
            v_t = v_loc[first_row:, group * width:(group + 1) * width].T
            op = jnp.concatenate([v_t, jnp.tile(t_loc[group], (1, 128 // width))], axis=1)
            gathered[group] = lax.all_gather(op, 'col', axis=0, tiled=True)
        x_t = lax.all_to_all(z_loc.T, 'row', 1, 0, tiled=True)
        for group in reversed(range(groups)):
            x_t = apply_group(x_t, gathered[group], group, width, row_devs)
        return x_t.T

    return jax.shard_map(local_apply, mesh=mesh,
                         in_specs=(P('row', 'col'), P('col', None, None), P(None, ('col', 'row'))),
                         out_specs=P('row', 'col'), check_vma=False)
```

time: 3380 us -> 440 us (0.13)
  matrix products: 1460 us -> 0 us
  blocking collectives: 1150 us -> 5.35 us
  waiting for transfers between devices: 720 us -> 192 us
  Pallas kernels: 0 us -> 218 us
    dot_general x576 -> x0, matrix products: 1460 us -> none  [the longest x192 765 us: panel_step(): jnp.einsum('na,nk->ak', v_j, x_in, precision=HIGHEST, preferred_element_t...]
    psum x192 -> x0, blocking collectives: 664 us -> none  [panel_step(): w_full = lax.psum(w_part, 'row')]
    all_gather x3, waiting for transfers between devices: 719 us -> 192 us  [local_apply(): gathered[group] = lax.all_gather(op, 'col', axis=0, tiled=True)]
    all_gather x3 -> x0, blocking collectives: 487 us -> none  [group_step(): t_group = lax.all_gather(t_blk, 'col', axis=0)]
    pallas_call x0 -> x3, Pallas kernels: none -> 218 us  [apply_group(): pl.pallas_call(functools.partial(group_kernel, dims), out_shape=jax.Shape...]
  transfers between devices with their start and end apart: 4 -> 3, of which waited for: 4 -> 3; matrix products, arithmetic and copies ran while one was open for 0% -> 1% of each run, Pallas kernels for 0% -> 29%
where the time goes in v1:
time: 440 us
  Pallas kernels  218 us (50%)
  waiting for transfers between devices  192 us (44%)
  between operations  13.2 us (3%)
  local copies, waits for them, and re-layouts  8.66 us (2%)
  blocking collectives  5.35 us (1%)
    pallas_call x3, Pallas kernels, apply_group(): pl.pallas_call(functools.partial(group_kernel, dims), out_shape=jax.Shape...  218 us
    all_gather x3, waiting for transfers between devices, local_apply(): gathered[group] = lax.all_gather(op, 'col', axis=0, tiled=True)  192 us
  transfers between devices with their start and end apart: 3, of which 3 were waited for; matrix products, arithmetic and copies ran while one was open for 1% of the time, Pallas kernels for 29%

profile of v1, /device:TPU:1, one launch (start us, length us, event | category | flops | bytes accessed | tf_op | source)
XLA Modules:
  0.0 440.1 jit_solution(7878023668373842145)
XLA Ops:
  6.5 0.0 all-gather.8.cloned.1.call-start
  6.5 0.8 slice_bitcast_fusion.3
  7.3 0.1 tile.38
  7.4 0.9 slice_bitcast_fusion.2
  8.3 0.7 pad_maximum_fusion.2
  9.0 0.0 all-gather.8.cloned.1.call-update
  9.0 0.0 all-gather.6.cloned.1.call-start
  9.1 0.1 tile.35
  9.2 1.0 slice_bitcast_fusion.1
  10.2 0.7 pad_maximum_fusion.1
  10.9 0.0 copy-start.1
  10.9 0.0 all-gather.6.cloned.1.call-update
  10.9 0.0 all-gather.4.cloned.1.call-start
  11.0 0.1 tile.32
  11.1 1.1 slice_bitcast_fusion
  12.2 0.8 pad_maximum_fusion
  12.9 0.0 all-gather.4.cloned.1.call-update
  13.0 0.0 copy-done.1
  13.0 0.1 copy.7
  13.0 5.4 %all_to_all.19 = f32[32,2,3072]{2,0,1:T(8,128)S(1)} all-to-all(f32[32,2,3072]{2,0,1:T(8,128)S(1)} %bitcast.23), channel_id=1, replica_groups=mesh['row'=2,'col'=64] {'row'}, dimensions={1} | all-to-all | bytes 1572864 | tf_op jit(solution)/shard_map/all_to_all | solution.py:132
  18.4 75.9 %all-gather.8.cloned.1.call-done.vt_hbm = f32[2048,1152]{1,0:T(8,128)} async-done(((f32[32,1152]{1,0:T(8,128)}), f32[2048,1152]{1,0:T(8,128)}) %all-gather.8.cloned.1.call-update) | async-done | bytes 9437200 | tf_op jit(solution)/shard_map/all_gather | solution.py:131
  94.3 0.0 copy-start
  94.3 3.7 copy-done
  98.0 54.1 %shard_map.37.xin_ref = f32[64,3072]{1,0:T(8,128)S(1)} custom-call(f32[2048,1152]{1,0:T(8,128)S(1)} %copy-done, f32[64,3072]{1,0:T(8,128)S(1)} %bitcast.21), custom_call_target="tpu_custom_call" | custom-call | flops 9663676416 | bytes 9437184 | tf_op jit(solution)/shard_map/pallas_call | solution.py:100
  152.0 51.5 %all-gather.6.cloned.1.call-done.vt_hbm = f32[2048,2176]{1,0:T(8,128)} async-done(((f32[32,2176]{1,0:T(8,128)}), f32[2048,2176]{1,0:T(8,128)}) %all-gather.6.cloned.1.call-update) | async-done | bytes 17825808 | tf_op jit(solution)/shard_map/all_gather | solution.py:131
  203.6 72.4 %shard_map.38.xin_ref = f32[64,3072]{1,0:T(8,128)S(1)} custom-call(f32[2048,2176]{1,0:T(8,128)} %all-gather.6.cloned.1.call-done.vt_hbm, f32[64,3072]{1,0:T(8,128)S(1)} %shard_map.37.xin_ref), custom_call_target="tpu_custom_call" | custom-call | flops 19327352832 | bytes 17825792 | tf_op jit(solution)/shard_map/pallas_call | solution.py:100
  276.0 64.9 %all-gather.4.cloned.1.call-done.vt_hbm = f32[2048,3200]{1,0:T(8,128)} async-done(((f32[32,3200]{1,0:T(8,128)}), f32[2048,3200]{1,0:T(8,128)}) %all-gather.4.cloned.1.call-update) | async-done | bytes 26214416 | tf_op jit(solution)/shard_map/all_gather | solution.py:131
  340.9 91.7 %shard_map.39 = f32[64,3072]{1,0:T(8,128)S(1)} custom-call(f32[2048,3200]{1,0:T(8,128)} %all-gather.4.cloned.1.call-done.vt_hbm, f32[64,3072]{1,0:T(8,128)S(1)} %shard_map.38.xin_ref), custom_call_target="tpu_custom_call" | custom-call | flops 28991029248 | bytes 26214400 | tf_op jit(solution)/shard_map/pallas_call | solution.py:100
  432.6 0.9 copy.9
  (3 shorter events, 0.0 us)
Async XLA Ops:
  6.5 87.8 %all-gather.8.cloned.1.call-start = ((), (), s32[]{:S(2)}) async-start(), calls=%async_computation.3 | async-start | bytes 9584640 | tf_op jit(solution)/shard_map/all_gather | solution.py:131
  9.0 194.5 %all-gather.6.cloned.1.call-start = ((), (), s32[]{:S(2)}) async-start(), calls=%async_computation.2 | async-start | bytes 18104320 | tf_op jit(solution)/shard_map/all_gather | solution.py:131
  10.9 2.1 copy-start.1
  10.9 330.0 %all-gather.4.cloned.1.call-start = ((), (), s32[]{:S(2)}) async-start(), calls=%async_computation.1 | async-start | bytes 26624000 | tf_op jit(solution)/shard_map/all_gather | solution.py:131
  94.3 3.7 copy-start
Sparse Core Ops, SparseCore 0:
  10.1 84.1 all-gather.7
  97.1 106.3 all-gather.5
  206.3 134.5 all-gather.3

commit v2 on v0

v2 whole, which is shorter than its diff:
```python
import functools

import jax
import jax.numpy as jnp
from jax import lax
from jax.experimental import pallas as pl
from jax.experimental.pallas import tpu as pltpu
from jax.sharding import PartitionSpec as P

HIGHEST = lax.Precision.HIGHEST
MESH = pl.DeviceIdType.MESH
BLOCK = 256
TILE = 128
CHUNK = 4
SIDE = 4
WIDTH = 32
TILES = {2: 8, 1: 16, 0: 24}
ORDERS = ((2, 1, 0), (1, 0, 2), (0, 2, 1))
RANGES = {
    2: ((7, 9), (0, 6), (6, 7)),
    1: ((13, 16), (0, 8), (8, 13)),
    0: ((17, 24), (0, 9), (9, 17)),
}


def dot_nn(a, b):
    return lax.dot_general(a, b, (((1,), (0,)), ((), ())), precision=HIGHEST, preferred_element_type=jnp.float32)


def dot_nt(a, b):
    return lax.dot_general(a, b, (((1,), (1,)), ((), ())), precision=HIGHEST, preferred_element_type=jnp.float32)


def regions(group, part, phase, coords, pos, half):
    order = ORDERS[part]
    low, high = RANGES[group][part]
    index = list(coords)
    index[order[phase]] = pos
    for axis in order[:phase]:
        index[axis] = pl.ds(0, SIDE)
    if half is not None:
        if phase == 0:
            middle = (low + high + 1) // 2
            low, high = ((low, middle), (middle, high))[half]
        else:
            index[order[0]] = pl.ds(2 * half, 2)
    if phase == 2 and part == 1:
        spans = [(z, max(low, 2 * z)) for z in range(SIDE)]
        return [(z, index[1], index[2], pl.ds(first, high - first)) for z, first in spans if first < high]
    if low == high:
        return []
    return [(*index, pl.ds(low, high - low))]


def semaphore_table():
    table = {}
    for group in TILES:
        for part in range(3):
            for phase in range(3):
                for stage in range(2):
                    for way in range(2):
                        half = way if stage else None
                        for i in range(len(regions(group, part, phase, (0, 0, 0), 0, half))):
                            table[group, part, phase, stage, way, i] = len(table)
    return table


TABLE = semaphore_table()


def kernel(v_hbm, t_tile, z_hbm, out_ref, buf2, buf1, buf0, x_buf, part_buf, other, load_sem, x_sem, send_sem, recv_sem,
           swap_send, swap_recv):
    bufs = {2: buf2, 1: buf1, 0: buf0}
    cols, local_rows = x_buf.shape
    share = cols // 2
    me = lax.axis_index('row')
    mate = 1 - me
    chip = lax.axis_index('col')
    coords = (chip // (SIDE * SIDE), lax.rem(chip // SIDE, SIDE), lax.rem(chip, SIDE))
    strides = (SIDE * SIDE, SIDE, 1)

    def shifted(axis, by):
        return lax.rem(coords[axis] + by + SIDE, SIDE)

    def neighbour(axis, by):
        return {'col': chip + (shifted(axis, by) - coords[axis]) * strides[axis]}

    for group in TILES:
        for z in range(1, SIDE):
            count = 2 * z
            shape = (SIDE, SIDE, count, WIDTH, TILE)
            bufs[group][z, :, :, 0:count, :, :] = jnp.zeros(shape, jnp.float32)

    barrier = pltpu.get_barrier_semaphore()
    pl.semaphore_signal(barrier, inc=1, device_id={'row': mate}, device_id_type=MESH)
    for axis in range(3):
        for by in (1, -1):
            pl.semaphore_signal(barrier, inc=1, device_id=neighbour(axis, by), device_id_type=MESH)
    pl.semaphore_wait(barrier, 7)

    own = {group: bufs[group].at[coords[0], coords[1], coords[2]] for group in TILES}
    for group, tiles in TILES.items():
        first = local_rows - tiles * TILE
        for tile in range(tiles):
            src = v_hbm.at[pl.ds(group * WIDTH, WIDTH), pl.ds(first + tile * TILE, TILE)]
            pltpu.make_async_copy(src, own[group].at[tile], load_sem.at[group]).start()
    pltpu.make_async_copy(t_tile, own[2].at[TILES[2]], load_sem.at[2]).start()

    keep = pltpu.make_async_copy(z_hbm.at[:, pl.ds(pl.multiple_of(me * local_rows, TILE), local_rows)],
                                 x_buf.at[pl.ds(pl.multiple_of(me * share, 8), share), :], x_sem.at[0])
    give = pltpu.make_async_remote_copy(
        src_ref=z_hbm.at[:, pl.ds(pl.multiple_of(mate * local_rows, TILE), local_rows)],
        dst_ref=x_buf.at[pl.ds(pl.multiple_of(me * share, 8), share), :],
        send_sem=x_sem.at[1], recv_sem=x_sem.at[2], device_id={'row': mate}, device_id_type=MESH)
    take = pltpu.make_async_remote_copy(
        src_ref=z_hbm.at[:, pl.ds(pl.multiple_of(mate * local_rows, TILE), local_rows)],
        dst_ref=x_buf.at[pl.ds(pl.multiple_of(mate * share, 8), share), :],
        send_sem=x_sem.at[1], recv_sem=x_sem.at[2], device_id={'row': mate}, device_id_type=MESH)

    def messages(group, phase, stage, incoming):
        copies = []
        for part in range(3):
            axis = ORDERS[part][phase]
            for way in range(2):
                sign = 1 - 2 * way
                behind = (-sign if stage else 0) + (-sign if incoming else 0)
                pos = shifted(axis, behind)
                half = way if stage else None
                for i, index in enumerate(regions(group, part, phase, coords, pos, half)):
                    number = TABLE[group, part, phase, stage, way, i]
                    ref = bufs[group].at[index]
                    copies.append(pltpu.make_async_remote_copy(
                        src_ref=ref, dst_ref=ref, send_sem=send_sem.at[number], recv_sem=recv_sem.at[number],
                        device_id=neighbour(axis, sign), device_id_type=MESH))
        return copies

    def send(group, phase, stage):
        for copy in messages(group, phase, stage, False):
            copy.start()

    def receive(group, phase, stage):
        for copy in messages(group, phase, stage, True):
            copy.wait_recv()

    def relay(group, phase, stage):
        receive(group, phase, stage)
        if stage == 0:
            send(group, phase, 1)
        elif phase < 2:
            send(group, phase + 1, 0)

    def loaded(group):
        pltpu.make_async_copy(own[group], own[group], load_sem.at[group]).wait()

    loaded(2)
    send(2, 0, 0)
    keep.start()
    give.start()
    loaded(1)
    loaded(0)
    relay(2, 0, 0)
    send(1, 0, 0)
    relay(2, 0, 1)
    relay(1, 0, 0)
    relay(2, 1, 0)
    send(0, 0, 0)
    relay(2, 1, 1)
    relay(1, 0, 1)
    relay(0, 0, 0)
    relay(2, 2, 0)
    relay(1, 1, 0)
    relay(1, 1, 1)
    relay(0, 0, 1)
    receive(2, 2, 1)
    keep.wait()
    take.wait_recv()

    row_id = lax.broadcasted_iota(jnp.int32, (BLOCK, BLOCK), 0)
    col_id = lax.broadcasted_iota(jnp.int32, (BLOCK, BLOCK), 1)

    def apply_group(group, events):
        buf = bufs[group]
        tiles = TILES[group]
        first_row = local_rows - tiles * TILE

        def block_step(step, carry):
            blk = 7 - step
            z, y = blk // 2, 2 * lax.rem(blk, 2)
            slot = lax.rem(step, 2)

            def tile_of(ref, tile):
                return ref[z, pl.ds(y, 2), :, tile].reshape(BLOCK, TILE)

            def chunk_of(c):
                return jnp.concatenate([tile_of(buf, c * CHUNK + i) for i in range(CHUNK)], axis=1)

            def rows_of(c):
                return pl.ds(pl.multiple_of(first_row + c * (CHUNK * TILE), TILE), CHUNK * TILE)

            start = blk // CHUNK
            part_buf[slot] = jnp.zeros(part_buf.shape[1:], jnp.float32)

            def products(c, carry):
                v_c = chunk_of(c)
                part_buf[slot] += dot_nt(jnp.concatenate([x_buf[:, rows_of(c)], v_c], axis=0), v_c)
                return carry

            lax.fori_loop(start, tiles // CHUNK, products, 0)

            swap = pltpu.make_async_remote_copy(
                src_ref=part_buf.at[slot], dst_ref=other.at[slot], send_sem=swap_send.at[slot],
                recv_sem=swap_recv.at[slot], device_id={'row': mate}, device_id_type=MESH)
            swap.start()
            swap.wait()

            w_t = part_buf[slot, :cols] + other[slot, :cols]
            gram = part_buf[slot, cols:] + other[slot, cols:]
            t_rows = tile_of(buf2, TILES[2])[:, group * WIDTH:(group + 1) * WIDTH]
            t_mat = jnp.concatenate([t_rows] * (BLOCK // WIDTH), axis=1)
            t_mat = jnp.where(row_id // WIDTH == col_id // WIDTH, t_mat, 0.0)
            size = WIDTH
            while size < BLOCK:
                pick = (row_id // size + 1 == col_id // size) & (row_id // (2 * size) == col_id // (2 * size))
                t_mat = t_mat - dot_nn(dot_nn(t_mat, jnp.where(pick, gram, 0.0)), t_mat)
                size *= 2
            y_t = dot_nt(w_t, t_mat)

            def update(c, carry):
                x_buf[:, rows_of(c)] -= dot_nn(y_t, chunk_of(c))
                return carry

            lax.fori_loop(start, tiles // CHUNK, update, 0)

            for when, event in events.items():
                @pl.when(step == when)
                def _():
                    relay(*event)

            return carry

        lax.fori_loop(0, 8, block_step, 0)

    apply_group(2, {1: (0, 1, 0), 3: (1, 2, 0), 5: (0, 1, 1)})
    receive(1, 2, 1)
    apply_group(1, {4: (0, 2, 0)})
    receive(0, 2, 1)
    apply_group(0, {})
    out_ref[...] = x_buf[...]

    give.wait_send()
    for group in TILES:
        for phase in range(3):
            for stage in range(2):
                for copy in messages(group, phase, stage, False):
                    copy.wait_send()


def solution(mesh):
    def local_apply(v_loc, t_loc, z_loc):
        groups, width = t_loc.shape[0], t_loc.shape[1]
        local_rows = v_loc.shape[0]
        share = z_loc.shape[1]
        t_tile = jnp.pad(t_loc.transpose(1, 0, 2).reshape(width, groups * width), ((0, 0), (0, TILE - groups * width)))
        cols = 2 * share
        any_spec = pl.BlockSpec(memory_space=pl.ANY)

        def buffer(tiles):
            return pltpu.VMEM((SIDE, SIDE, SIDE, tiles, WIDTH, TILE), jnp.float32)

        x_t = pl.pallas_call(
            kernel,
            out_shape=jax.ShapeDtypeStruct((cols, local_rows), jnp.float32),
            in_specs=[any_spec, any_spec, any_spec],
            out_specs=pl.BlockSpec(memory_space=pltpu.VMEM),
            scratch_shapes=[
                buffer(TILES[2] + 1),
                buffer(TILES[1]),
                buffer(TILES[0]),
                pltpu.VMEM((cols, local_rows), jnp.float32),
                pltpu.VMEM((2, cols + BLOCK, BLOCK), jnp.float32),
                pltpu.VMEM((2, cols + BLOCK, BLOCK), jnp.float32),
                pltpu.SemaphoreType.DMA((3,)),
                pltpu.SemaphoreType.DMA((3,)),
                pltpu.SemaphoreType.DMA((len(TABLE),)),
                pltpu.SemaphoreType.DMA((len(TABLE),)),
                pltpu.SemaphoreType.DMA((2,)),
                pltpu.SemaphoreType.DMA((2,)),
            ],
            compiler_params=pltpu.CompilerParams(collective_id=0, has_side_effects=True, vmem_limit_bytes=67043328),
        )(v_loc.T, t_tile, z_loc.T)
        return x_t.T

    return jax.shard_map(local_apply, mesh=mesh,
                         in_specs=(P('row', 'col'), P('col', None, None), P(None, ('col', 'row'))),
                         out_specs=P('row', 'col'), check_vma=False)
```

time: 3380 us -> 317 us (0.09)
  matrix products: 1460 us -> 0 us
  blocking collectives: 1150 us -> 0 us
  waiting for transfers between devices: 720 us -> 0 us
  Pallas kernels: 0 us -> 312 us
    dot_general x576 -> x0, matrix products: 1460 us -> none  [the longest x192 765 us: panel_step(): jnp.einsum('na,nk->ak', v_j, x_in, precision=HIGHEST, preferred_element_t...]
    all_gather x3 -> x0, waiting for transfers between devices: 719 us -> none  [group_step(): v_group = lax.all_gather(v_blk, 'col', axis=0)]
    psum x192 -> x0, blocking collectives: 664 us -> none  [panel_step(): w_full = lax.psum(w_part, 'row')]
    all_gather x3 -> x0, blocking collectives: 487 us -> none  [group_step(): t_group = lax.all_gather(t_blk, 'col', axis=0)]
    pallas_call x0 -> x1, Pallas kernels: none -> 312 us  [local_apply(): pl.pallas_call(kernel, out_shape=jax.ShapeDtypeStruct((cols, local_rows),...]
  transfers between devices with their start and end apart: 4 -> 0, of which waited for: 4 -> 0; matrix products, arithmetic and copies ran while one was open for 0% -> 0% of each run, Pallas kernels for 0% -> 0%
where the time goes in v2:
time: 317 us; the launch traced here: 316 us
  Pallas kernels  312 us (98%)
  local copies, waits for them, and re-layouts  3.61 us (1%)
    pallas_call x1, Pallas kernels, local_apply(): pl.pallas_call(kernel, out_shape=jax.ShapeDtypeStruct((cols, local_rows),...  312 us

profile of v2, /device:TPU:1, one launch (start us, length us, event | category | flops | bytes accessed | tf_op | source)
XLA Modules:
  0.0 315.7 jit_solution(17783229157808391300)
XLA Ops:
  0.0 0.8 copy.5
  0.8 0.1 reshape.3
  0.9 0.6 pad.4.t_tile
  1.5 312.1 %shard_map.37 = f32[64,3072]{1,0:T(8,128)} custom-call(f32[96,3072]{1,0:T(8,128)} %bitcast.5, f32[32,128]{1,0:T(8,128)} %pad.4.t_tile, f32[32,6144]{1,0:T(8,128)} %bitcast.6), custom_call_target="tpu_custom_call" | custom-call | tf_op jit(solution)/shard_map/pallas_call | solution.py:270
  313.7 2.1 copy.7

commit v3 on v0

v3 whole, which is shorter than its diff:
```python
import functools

import jax
import jax.numpy as jnp
from jax import lax
from jax.experimental import pallas as pl
from jax.experimental.pallas import tpu as pltpu
from jax.sharding import PartitionSpec as P

HIGHEST = lax.Precision.HIGHEST
MESH = pl.DeviceIdType.MESH
BLOCK = 256
HALF = BLOCK // 2
TILE = 128
CHUNK = 4
SIDE = 4
WIDTH = 32
TILES = {2: 8, 1: 16, 0: 24}
EXTRA = {2: 1, 1: 0, 0: 1}
OWNER = 0
QUARTER = TILES[OWNER] // SIDE * TILE
ORDERS = ((2, 1, 0), (1, 0, 2), (0, 2, 1))
RANGES = {
    2: ((7, 9), (0, 6), (6, 7)),
    1: ((12, 16), (0, 8), (8, 12)),
    0: ((20, 25), (0, 11), (11, 20)),
}
STREAMED = 0


def dot_nn(a, b):
    return lax.dot_general(a, b, (((1,), (0,)), ((), ())), precision=HIGHEST, preferred_element_type=jnp.float32)


def dot_nt(a, b):
    return lax.dot_general(a, b, (((1,), (1,)), ((), ())), precision=HIGHEST, preferred_element_type=jnp.float32)


def regions(group, part, phase, plane, coords, pos, half):
    order = ORDERS[part]
    low, high = RANGES[group][part]
    index = list(coords)
    index[order[phase]] = pos
    for axis in order[:phase]:
        index[axis] = pl.ds(0, SIDE)
    if phase == 0:
        middle = (low + high + 1) // 2
        low, high = ((low, middle), (middle, high))[half]
    else:
        index[order[1 if plane is not None and order[0] == 0 else 0]] = pl.ds(2 * half, 2)
    if phase == 2 and part > 0 and (part == 1 or plane is not None):
        planes = range(SIDE) if plane is None else (plane,)
        spans = [(z, max(low, 2 * z) if part == 1 else low) for z in planes]
        return [(z, index[1], index[2], pl.ds(first, high - first)) for z, first in spans if first < high]
    if low == high:
        return []
    return [(*index, pl.ds(low, high - low))]


def parts_of(group, phase, plane):
    if group != STREAMED or phase < 2:
        return (0, 1, 2)
    return (0,) if plane is None else (1, 2)


def planes_of(group, phase):
    return (None, 3, 2, 1, 0) if group == STREAMED and phase == 2 else (None,)


def message_keys():
    for group in TILES:
        for phase in range(3):
            for plane in planes_of(group, phase):
                for piece in range(3):
                    yield group, phase, plane, piece


def half_of(piece, way):
    return 1 - way if piece == 1 else way


def semaphore_table():
    table = {}
    for group, phase, plane, piece in message_keys():
        for part in parts_of(group, phase, plane):
            for way in range(2):
                for i in range(len(regions(group, part, phase, plane, (0, 0, 0), 0, half_of(piece, way)))):
                    table[group, phase, plane, piece, part, way, i] = len(table)
    return table


TABLE = semaphore_table()


def kernel(v_hbm, t_hbm, z_hbm, out_ref, buf2, buf1, buf0, x_buf, w_part, w_other, g_part, g_other, quarters, t_line,
           line_part, line_other, line_half, line_gram, line_t,
           load_sem, x_sem, send_sem, recv_sem, swap_send, swap_recv, line_send, line_recv, line_load):
    bufs = {2: buf2, 1: buf1, 0: buf0}
    cols, local_rows = x_buf.shape
    share = cols // 2
    me = lax.axis_index('row')
    mate = 1 - me
    chip = lax.axis_index('col')
    coords = (chip // (SIDE * SIDE), lax.rem(chip // SIDE, SIDE), lax.rem(chip, SIDE))
    strides = (SIDE * SIDE, SIDE, 1)
    my_x = coords[2]

    def shifted(axis, by):
        return lax.rem(coords[axis] + by + SIDE, SIDE)

    def neighbour(axis, by):
        return {'col': chip + (shifted(axis, by) - coords[axis]) * strides[axis]}

    def to_mate(src, dst, send, recv):
        return pltpu.make_async_remote_copy(src_ref=src, dst_ref=dst, send_sem=send, recv_sem=recv,
                                            device_id={'row': mate}, device_id_type=MESH)

    for group in TILES:
        for z in range(1, SIDE):
            shape = (SIDE, SIDE, 2 * z, WIDTH, TILE)
            bufs[group][z, :, :, 0:2 * z, :, :] = jnp.zeros(shape, jnp.float32)

    barrier = pltpu.get_barrier_semaphore()
    pl.semaphore_signal(barrier, inc=1, device_id={'row': mate}, device_id_type=MESH)
    for axis, by in ((0, 1), (0, -1), (1, 1), (1, -1), (2, 1), (2, 2), (2, 3)):
        pl.semaphore_signal(barrier, inc=1, device_id=neighbour(axis, by), device_id_type=MESH)
    pl.semaphore_wait(barrier, 8)

    own = {group: bufs[group].at[coords[0], coords[1], coords[2]] for group in TILES}

    def load(group):
        first = local_rows - TILES[group] * TILE
        for tile in range(TILES[group]):
            src = v_hbm.at[pl.ds(group * WIDTH, WIDTH), pl.ds(first + tile * TILE, TILE)]
            pltpu.make_async_copy(src, own[group].at[tile], load_sem.at[group]).start()
        if group == 2:
            pltpu.make_async_copy(t_hbm, own[2].at[TILES[2]], load_sem.at[2]).start()

    def loaded(group):
        tiles = pl.ds(0, TILES[group] + (1 if group == 2 else 0))
        pltpu.make_async_copy(own[group].at[tiles], own[group].at[tiles], load_sem.at[group]).wait()

    mine = pl.ds(pl.multiple_of(me * local_rows, TILE), local_rows)
    theirs = pl.ds(pl.multiple_of(mate * local_rows, TILE), local_rows)
    my_cols = x_buf.at[pl.ds(pl.multiple_of(me * share, 8), share), :]
    their_cols = x_buf.at[pl.ds(pl.multiple_of(mate * share, 8), share), :]
    keep = pltpu.make_async_copy(z_hbm.at[:, mine], my_cols, x_sem.at[0])
    give = to_mate(z_hbm.at[:, theirs], my_cols, x_sem.at[1], x_sem.at[2])
    take = to_mate(z_hbm.at[:, theirs], their_cols, x_sem.at[1], x_sem.at[2])

    def messages(group, phase, plane, piece, incoming):
        copies = []
        for part in parts_of(group, phase, plane):
            axis = ORDERS[part][phase]
            for way in range(2):
                sign = 1 - 2 * way
                pos = shifted(axis, (-sign if piece == 2 else 0) + (-sign if incoming else 0))
                for i, index in enumerate(regions(group, part, phase, plane, coords, pos, half_of(piece, way))):
                    number = TABLE[group, phase, plane, piece, part, way, i]
                    ref = bufs[group].at[index]
                    copies.append(pltpu.make_async_remote_copy(
                        src_ref=ref, dst_ref=ref, send_sem=send_sem.at[number], recv_sem=recv_sem.at[number],
                        device_id=neighbour(axis, sign), device_id_type=MESH))
        return copies

    def begin(group, phase, plane=None):
        for piece in range(2):
            for copy in messages(group, phase, plane, piece, False):
                copy.start()

    def forward(group, phase, plane=None):
        for copy in messages(group, phase, plane, 0, True):
            copy.wait_recv()
        for copy in messages(group, phase, plane, 2, False):
            copy.start()

    def finish(group, phase, plane=None):
        for piece in range(1, 3):
            for copy in messages(group, phase, plane, piece, True):
                copy.wait_recv()

    def advance(group, phase):
        finish(group, phase)
        begin(group, phase + 1)
        if group == STREAMED and phase == 1:
            begin(group, 2, 3)
            begin(group, 2, 2)

    def quarter(x):
        return v_hbm.at[pl.ds(OWNER * WIDTH, WIDTH), pl.ds(pl.multiple_of(x * QUARTER, TILE), QUARTER)]

    def line_copies(kind, incoming):
        copies = []
        for by in range(1, SIDE):
            other = shifted(2, by)
            slot = shifted(2, -by) if incoming else my_x
            src, dst = {
                0: (quarter(other), quarters.at[slot]),
                1: (t_hbm, t_line.at[slot]),
                2: (line_half.at[my_x], line_half.at[slot]),
            }[kind]
            copies.append(pltpu.make_async_remote_copy(
                src_ref=src, dst_ref=dst, send_sem=line_send.at[kind, by - 1], recv_sem=line_recv.at[kind, by - 1],
                device_id=neighbour(2, by), device_id_type=MESH))
        return copies

    own_quarter = pltpu.make_async_copy(quarter(my_x), quarters.at[my_x], line_load.at[0])
    own_t = pltpu.make_async_copy(t_hbm, t_line.at[my_x], line_load.at[1])
    swap_line = to_mate(line_part, line_other, line_send.at[3, 0], line_recv.at[3, 0])
    my_half = pl.ds(pl.multiple_of(me * (HALF // 2), 8), HALF // 2)
    their_half = pl.ds(pl.multiple_of(mate * (HALF // 2), 8), HALF // 2)
    give_half = to_mate(line_gram.at[my_half, :], line_gram.at[my_half, :], line_send.at[3, 1], line_recv.at[3, 1])
    take_half = to_mate(line_gram.at[my_half, :], line_gram.at[their_half, :], line_send.at[3, 1], line_recv.at[3, 1])

    def block_diagonal(t_rows, group):
        size = t_rows.shape[0]
        column = t_rows[:, group * WIDTH:(group + 1) * WIDTH]
        wide = jnp.concatenate([column] * (size // WIDTH), axis=1)
        row_id = lax.broadcasted_iota(jnp.int32, (size, size), 0)
        col_id = lax.broadcasted_iota(jnp.int32, (size, size), 1)
        return jnp.where(row_id // WIDTH == col_id // WIDTH, wide, 0.0), row_id, col_id

    def merged(t_rows, group, gram):
        t_mat, row_id, col_id = block_diagonal(t_rows, group)
        size = WIDTH
        while size < gram.shape[0]:
            pick = (row_id // size + 1 == col_id // size) & (row_id // (2 * size) == col_id // (2 * size))
            t_mat = t_mat - dot_nn(dot_nn(t_mat, jnp.where(pick, gram, 0.0)), t_mat)
            size *= 2
        return t_mat

    def line_1():
        for kind in range(2):
            for copy in line_copies(kind, True):
                copy.wait_recv()
        own_quarter.wait()
        own_t.wait()
        q = quarters[...].reshape(HALF, QUARTER)
        line_part[...] = dot_nt(q, q)
        swap_line.start()

    def line_2():
        swap_line.wait_recv()
        line_half[my_x] = line_part[my_half, :] + line_other[my_half, :]
        for copy in line_copies(2, False):
            copy.start()

    def line_3():
        for copy in line_copies(2, True):
            copy.wait_recv()
        line_gram[my_half, :] = (line_half[0] + line_half[1]) + (line_half[2] + line_half[3])
        give_half.start()

    def line_4():
        take_half.wait_recv()
        line_t[...] = merged(t_line[...].reshape(HALF, TILE), OWNER, line_gram[...])
        bufs[OWNER][coords[0], coords[1], coords[2], TILES[OWNER]] = line_t[pl.ds(pl.multiple_of(my_x * WIDTH, 8), WIDTH), :]

    load(2)
    for kind in range(2):
        for copy in line_copies(kind, False):
            copy.start()
    own_quarter.start()
    own_t.start()
    load(1)
    loaded(2)
    begin(2, 0)
    load(0)
    keep.start()
    give.start()
    loaded(1)
    begin(1, 0)
    loaded(0)
    forward(2, 0)
    line_1()
    forward(1, 0)
    advance(2, 0)
    line_2()
    line_3()
    line_4()
    forward(2, 1)
    advance(2, 1)
    begin(0, 0)
    advance(1, 0)
    forward(2, 2)
    forward(0, 0)
    forward(1, 1)
    finish(2, 2)
    keep.wait()
    take.wait_recv()

    def apply_group(group, before, middle):
        buf = bufs[group]
        tiles = TILES[group]
        first_row = local_rows - tiles * TILE

        def block_step(step, carry):
            blk = 7 - step
            z, y = blk // 2, 2 * lax.rem(blk, 2)
            slot = lax.rem(step, 2)

            for when, events in before.items():
                @pl.when(step == when)
                def _():
                    for event in events:
                        event()

            def run_middle():
                for when, events in middle.items():
                    @pl.when(step == when)
                    def _():
                        for event in events:
                            event()

            def chunk_of(c):
                pieces = [buf[z, pl.ds(y, 2), :, c * CHUNK + i].reshape(BLOCK, TILE) for i in range(CHUNK)]
                return jnp.concatenate(pieces, axis=1)

            def rows_of(c):
                return pl.ds(pl.multiple_of(first_row + c * (CHUNK * TILE), TILE), CHUNK * TILE)

            def over_chunks(body):
                lax.fori_loop(blk // CHUNK, tiles // CHUNK, lambda c, carry: (body(c), carry)[1], 0)

            if group == OWNER:
                w_part[slot] = jnp.zeros(w_part.shape[1:], jnp.float32)

                def products(c):
                    v_c = chunk_of(c)
                    w_part[slot] += dot_nt(jnp.concatenate([x_buf[:, rows_of(c)], v_c[:HALF]], axis=0), v_c)

                over_chunks(products)
                swap = to_mate(w_part.at[slot], w_other.at[slot], swap_send.at[0, slot], swap_recv.at[0, slot])
                swap.start()
                run_middle()
                swap.wait()
                total = w_part[slot] + w_other[slot]
                w_1, w_2 = total[:cols, :HALF], total[:cols, HALF:]
                cross = total[cols:, HALF:]
                t_1 = buf[z, y, :, tiles].reshape(HALF, TILE)
                t_2 = buf[z, y + 1, :, tiles].reshape(HALF, TILE)
                y_2 = dot_nt(w_2, t_2)
                y_1 = dot_nt(w_1 - dot_nt(y_2, cross), t_1)
                y_t = jnp.concatenate([y_1, y_2], axis=1)
            else:
                g_part[slot] = jnp.zeros(g_part.shape[1:], jnp.float32)

                def gram_products(c):
                    v_c = chunk_of(c)
                    g_part[slot] += dot_nt(v_c, v_c)

                over_chunks(gram_products)
                g_swap = to_mate(g_part.at[slot], g_other.at[slot], swap_send.at[1, slot], swap_recv.at[1, slot])
                g_swap.start()
                w_rows = pl.ds(0, cols)
                w_part[slot, w_rows] = jnp.zeros((cols, BLOCK), jnp.float32)

                def w_products(c):
                    w_part[slot, w_rows] += dot_nt(x_buf[:, rows_of(c)], chunk_of(c))

                over_chunks(w_products)
                swap = to_mate(w_part.at[slot, w_rows], w_other.at[slot, w_rows], swap_send.at[0, slot], swap_recv.at[0, slot])
                swap.start()
                g_swap.wait()
                t_rows = buf2[z, pl.ds(y, 2), :, TILES[2]].reshape(BLOCK, TILE)
                t_mat = merged(t_rows, group, g_part[slot] + g_other[slot])
                run_middle()
                swap.wait()
                y_t = dot_nt(w_part[slot, w_rows] + w_other[slot, w_rows], t_mat)

            def update(c):
                x_buf[:, rows_of(c)] -= dot_nn(y_t, chunk_of(c))

            over_chunks(update)
            return carry

        lax.fori_loop(0, 8, block_step, 0)

    act = functools.partial
    apply_group(2, {1: [act(advance, 0, 0)], 2: [act(advance, 1, 1)], 6: [act(forward, 0, 1)]}, {})
    forward(1, 2)
    advance(0, 1)
    finish(1, 2)
    apply_group(1, {}, {
        3: [act(forward, 0, 2, 3), act(begin, 0, 2, 1)],
        4: [act(forward, 0, 2), act(forward, 0, 2, 2), act(begin, 0, 2, 0)],
        7: [act(forward, 0, 2, 1)],
    })
    finish(0, 2)
    finish(0, 2, 3)
    apply_group(0, {2: [act(finish, 0, 2, 2)], 4: [act(finish, 0, 2, 1)], 6: [act(finish, 0, 2, 0)]},
                {0: [act(forward, 0, 2, 0)]})
    out_ref[...] = x_buf[...]

    give.wait_send()
    swap_line.wait_send()
    give_half.wait_send()
    for kind in range(3):
        for copy in line_copies(kind, False):
            copy.wait_send()
    for key in message_keys():
        for copy in messages(*key, False):
            copy.wait_send()


def solution(mesh):
    def local_apply(v_loc, t_loc, z_loc):
        groups, width = t_loc.shape[0], t_loc.shape[1]
        local_rows = v_loc.shape[0]
        cols = 2 * z_loc.shape[1]
        t_tile = jnp.pad(t_loc.transpose(1, 0, 2).reshape(width, groups * width), ((0, 0), (0, TILE - groups * width)))
        any_spec = pl.BlockSpec(memory_space=pl.ANY)
        dma = pltpu.SemaphoreType.DMA

        def vmem(*shape):
            return pltpu.VMEM(shape, jnp.float32)

        x_t = pl.pallas_call(
            kernel,
            out_shape=jax.ShapeDtypeStruct((cols, local_rows), jnp.float32),
            in_specs=[any_spec, any_spec, any_spec],
            out_specs=pl.BlockSpec(memory_space=pltpu.VMEM),
            scratch_shapes=[
                *(vmem(SIDE, SIDE, SIDE, TILES[group] + EXTRA[group], WIDTH, TILE) for group in (2, 1, 0)),
                vmem(cols, local_rows),
                vmem(2, cols + HALF, BLOCK), vmem(2, cols + HALF, BLOCK),
                vmem(2, BLOCK, BLOCK), vmem(2, BLOCK, BLOCK),
                vmem(SIDE, WIDTH, QUARTER), vmem(SIDE, WIDTH, TILE),
                vmem(HALF, HALF), vmem(HALF, HALF), vmem(SIDE, HALF // 2, HALF), vmem(HALF, HALF), vmem(HALF, HALF),
                dma((3,)), dma((3,)), dma((len(TABLE),)), dma((len(TABLE),)), dma((2, 2)), dma((2, 2)),
                dma((4, 3)), dma((4, 3)), dma((2,)),
            ],
            compiler_params=pltpu.CompilerParams(collective_id=0, has_side_effects=True, vmem_limit_bytes=67043328),
        )(v_loc.T, t_tile, z_loc.T)
        return x_t.T

    return jax.shard_map(local_apply, mesh=mesh,
                         in_specs=(P('row', 'col'), P('col', None, None), P(None, ('col', 'row'))),
                         out_specs=P('row', 'col'), check_vma=False)
```

time: 3380 us -> 288 us (0.09)
  matrix products: 1460 us -> 0 us
  blocking collectives: 1150 us -> 0 us
  waiting for transfers between devices: 720 us -> 0 us
  Pallas kernels: 0 us -> 284 us
    dot_general x576 -> x0, matrix products: 1460 us -> none  [the longest x192 765 us: panel_step(): jnp.einsum('na,nk->ak', v_j, x_in, precision=HIGHEST, preferred_element_t...]
    all_gather x3 -> x0, waiting for transfers between devices: 719 us -> none  [group_step(): v_group = lax.all_gather(v_blk, 'col', axis=0)]
    psum x192 -> x0, blocking collectives: 664 us -> none  [panel_step(): w_full = lax.psum(w_part, 'row')]
    all_gather x3 -> x0, blocking collectives: 487 us -> none  [group_step(): t_group = lax.all_gather(t_blk, 'col', axis=0)]
    pallas_call x0 -> x1, Pallas kernels: none -> 284 us  [local_apply(): pl.pallas_call(kernel, out_shape=jax.ShapeDtypeStruct((cols, local_rows),...]
  transfers between devices with their start and end apart: 4 -> 0, of which waited for: 4 -> 0; matrix products, arithmetic and copies ran while one was open for 0% -> 0% of each run, Pallas kernels for 0% -> 0%
where the time goes in v3:
time: 288 us
  Pallas kernels  284 us (99%)
  local copies, waits for them, and re-layouts  3.61 us (1%)
    pallas_call x1, Pallas kernels, local_apply(): pl.pallas_call(kernel, out_shape=jax.ShapeDtypeStruct((cols, local_rows),...  284 us

profile of v3, /device:TPU:1, one launch (start us, length us, event | category | flops | bytes accessed | tf_op | source)
XLA Modules:
  0.0 287.8 jit_solution(8262590809171859731)
XLA Ops:
  0.0 0.8 copy.5
  0.8 0.1 reshape.3
  0.9 0.6 pad.4.t_hbm
  1.5 284.2 %shard_map.37 = f32[64,3072]{1,0:T(8,128)} custom-call(f32[96,3072]{1,0:T(8,128)} %bitcast.5, f32[32,128]{1,0:T(8,128)} %pad.4.t_hbm, f32[32,6144]{1,0:T(8,128)} %bitcast.6), custom_call_target="tpu_custom_call" | custom-call | tf_op jit(solution)/shard_map/pallas_call | solution.py:418
  285.7 2.1 copy.7

commit v4 on v3

v4 whole, which is shorter than its diff:
```python
import jax
import jax.numpy as jnp
from jax import lax
from jax.experimental import pallas as pl
from jax.experimental.pallas import tpu as pltpu
from jax.sharding import PartitionSpec as P

HIGHEST = lax.Precision.HIGHEST
MESH = pl.DeviceIdType.MESH
BLOCK = 256
HALF = BLOCK // 2
TILE = 128
SIDE = 4
WIDTH = 32
TILES = {2: 8, 1: 16, 0: 24}
EXTRA = {2: 1, 1: 0, 0: 0}
OWNERS = (1, 0)
ROUND_T = 3
QUARTERS = {group: TILES[group] // SIDE * TILE for group in OWNERS}
ORDERS = ((2, 1, 0), (1, 0, 2), (0, 2, 1))
RANGES = {
    2: ((7, 9), (0, 3), (3, 7)),
    1: ((12, 16), (0, 7), (7, 12)),
    0: ((18, 24), (0, 10), (10, 18)),
    3: ((0, 0), (0, 1), (1, 2)),
}
ROUNDS = (2, 1, 0, ROUND_T)
PRELUDE = (
    'L1 f20 f10 L2', 'f00 e20 b21 e10', 'b11 L3 e00 L4', 'b30 f21 f11 f30', 'e21 b22 b223 b222',
    'b221 f223 e11 e30', 'b31 f222 f22 b220', 'f221 e223 b12 f31', 'b01 e222 f220 e22',
)
EVENTS = {
    (2, 'before'): {3: 'e220', 5: 'f122', 6: 'e123', 7: 'f32'},
    (2, 'mid'): {0: 'e221', 1: 'b123', 2: 'f12', 3: 'b122 f123', 4: 'e31', 5: 'b32 f01', 6: 'e122', 7: 'b121'},
    (1, 'before'): {0: 'e32 e12', 2: 'f120', 5: 'f02 f023'},
    (1, 'mid'): {0: 'b120 f121', 1: 'e01 b02', 3: 'e121 b023', 4: 'e120', 5: 'b022', 6: 'e023', 7: 'f022'},
    (0, 'before'): {0: 'b021 e022 b020 f021 e02', 4: 'e021', 6: 'e020'},
    (0, 'mid'): {1: 'f020'},
}


def dot_nn(a, b):
    return lax.dot_general(a, b, (((1,), (0,)), ((), ())), precision=HIGHEST, preferred_element_type=jnp.float32)


def dot_nt(a, b):
    return lax.dot_general(a, b, (((1,), (1,)), ((), ())), precision=HIGHEST, preferred_element_type=jnp.float32)


def regions(group, part, phase, plane, coords, pos, half):
    order = ORDERS[part]
    low, high = RANGES[group][part]
    index = list(coords)
    index[order[phase]] = pos
    for axis in order[:phase]:
        index[axis] = pl.ds(0, SIDE)
    if phase == 0:
        middle = (low + high + 1) // 2
        low, high = ((low, middle), (middle, high))[half]
    else:
        index[order[1 if plane is not None and order[0] == 0 else 0]] = pl.ds(2 * half, 2)
    if plane is not None:
        index[0] = plane
        low = max(low, 2 * plane)
    return (*index, pl.ds(low, high - low)) if low < high else None


def planes_of(group, phase):
    return (None, 3, 2, 1, 0) if phase == 2 and group != ROUND_T else (None,)


def parts_of(group, phase, plane):
    if planes_of(group, phase) == (None,):
        return (0, 1, 2)
    return (0,) if plane is None else (1, 2)


def message_keys():
    for group in ROUNDS:
        for phase in range(3):
            for plane in planes_of(group, phase):
                for piece in range(3):
                    yield group, phase, plane, piece


def half_of(piece, way):
    return 1 - way if piece == 1 else way


def semaphore_table():
    table = {}
    for group, phase, plane, piece in message_keys():
        for part in parts_of(group, phase, plane):
            for way in range(2):
                if regions(group, part, phase, plane, (0, 0, 0), 0, half_of(piece, way)) is not None:
                    table[group, phase, plane, piece, part, way] = len(table)
    return table


TABLE = semaphore_table()


def kernel(v_hbm, t_hbm, z_hbm, out_ref, buf2, buf1, buf0, buf_t, x_buf, w_part, w_other, g_part, g_other, quarters_1,
           quarters_0, t_line,
           line_part, line_other, line_half, line_gram, line_t,
           load_sem, x_sem, send_sem, recv_sem, swap_send, swap_recv, line_send, line_recv, line_load):
    bufs = {2: buf2, 1: buf1, 0: buf0, ROUND_T: buf_t}
    quarters = {1: quarters_1, 0: quarters_0}
    cols, local_rows = x_buf.shape
    share = cols // 2
    me = lax.axis_index('row')
    mate = 1 - me
    chip = lax.axis_index('col')
    coords = (chip // (SIDE * SIDE), lax.rem(chip // SIDE, SIDE), lax.rem(chip, SIDE))
    strides = (SIDE * SIDE, SIDE, 1)
    my_x = coords[2]

    def shifted(axis, by):
        return lax.rem(coords[axis] + by + SIDE, SIDE)

    def neighbour(axis, by):
        return {'col': chip + (shifted(axis, by) - coords[axis]) * strides[axis]}

    def to_mate(src, dst, send, recv):
        return pltpu.make_async_remote_copy(src_ref=src, dst_ref=dst, send_sem=send, recv_sem=recv,
                                            device_id={'row': mate}, device_id_type=MESH)

    for group in TILES:
        for z in range(1, SIDE):
            shape = (SIDE, SIDE, 2 * z, WIDTH, TILE)
            bufs[group][z, :, :, 0:2 * z, :, :] = jnp.zeros(shape, jnp.float32)

    barrier = pltpu.get_barrier_semaphore()
    pl.semaphore_signal(barrier, inc=1, device_id={'row': mate}, device_id_type=MESH)
    for axis, by in ((0, 1), (0, -1), (1, 1), (1, -1), (2, 1), (2, 2), (2, 3)):
        pl.semaphore_signal(barrier, inc=1, device_id=neighbour(axis, by), device_id_type=MESH)
    pl.semaphore_wait(barrier, 8)

    own = {group: bufs[group].at[coords[0], coords[1], coords[2]] for group in TILES}

    def load(group):
        first = local_rows - TILES[group] * TILE
        for tile in range(TILES[group]):
            src = v_hbm.at[pl.ds(group * WIDTH, WIDTH), pl.ds(first + tile * TILE, TILE)]
            pltpu.make_async_copy(src, own[group].at[tile], load_sem.at[group]).start()
        if group == 2:
            pltpu.make_async_copy(t_hbm, own[2].at[TILES[2]], load_sem.at[2]).start()

    def loaded(group):
        tiles = pl.ds(0, TILES[group] + (1 if group == 2 else 0))
        pltpu.make_async_copy(own[group].at[tiles], own[group].at[tiles], load_sem.at[group]).wait()

    mine = pl.ds(pl.multiple_of(me * local_rows, TILE), local_rows)
    theirs = pl.ds(pl.multiple_of(mate * local_rows, TILE), local_rows)
    my_cols = x_buf.at[pl.ds(pl.multiple_of(me * share, 8), share), :]
    their_cols = x_buf.at[pl.ds(pl.multiple_of(mate * share, 8), share), :]
    keep = pltpu.make_async_copy(z_hbm.at[:, mine], my_cols, x_sem.at[0])
    give = to_mate(z_hbm.at[:, theirs], my_cols, x_sem.at[1], x_sem.at[2])
    take = to_mate(z_hbm.at[:, theirs], their_cols, x_sem.at[1], x_sem.at[2])

    def messages(group, phase, plane, piece, incoming):
        copies = []
        for part in parts_of(group, phase, plane):
            axis = ORDERS[part][phase]
            for way in range(2):
                sign = 1 - 2 * way
                pos = shifted(axis, (-sign if piece == 2 else 0) + (-sign if incoming else 0))
                index = regions(group, part, phase, plane, coords, pos, half_of(piece, way))
                if index is None:
                    continue
                number = TABLE[group, phase, plane, piece, part, way]
                ref = bufs[group].at[index]
                copies.append(pltpu.make_async_remote_copy(
                    src_ref=ref, dst_ref=ref, send_sem=send_sem.at[number], recv_sem=recv_sem.at[number],
                    device_id=neighbour(axis, sign), device_id_type=MESH))
        return copies

    def begin(group, phase, plane=None):
        for piece in range(2):
            for copy in messages(group, phase, plane, piece, False):
                copy.start()

    def forward(group, phase, plane=None):
        for copy in messages(group, phase, plane, 0, True):
            copy.wait_recv()
        for copy in messages(group, phase, plane, 2, False):
            copy.start()

    def finish(group, phase, plane=None):
        for piece in range(1, 3):
            for copy in messages(group, phase, plane, piece, True):
                copy.wait_recv()

    def quarter(group, x):
        first = local_rows - TILES[group] * TILE
        lanes = pl.ds(pl.multiple_of(first + x * QUARTERS[group], TILE), QUARTERS[group])
        return v_hbm.at[pl.ds(group * WIDTH, WIDTH), lanes]

    def line_copies(kind, incoming):
        copies = []
        for by in range(1, SIDE):
            other = shifted(2, by)
            slot = shifted(2, -by) if incoming else my_x
            if kind < 2:
                src, dst = quarter(OWNERS[kind], other), quarters[OWNERS[kind]].at[slot]
            elif kind == 2:
                src, dst = t_hbm, t_line.at[slot]
            else:
                src, dst = line_half.at[my_x], line_half.at[slot]
            copies.append(pltpu.make_async_remote_copy(
                src_ref=src, dst_ref=dst, send_sem=line_send.at[kind, by - 1], recv_sem=line_recv.at[kind, by - 1],
                device_id=neighbour(2, by), device_id_type=MESH))
        return copies

    own_copies = [pltpu.make_async_copy(quarter(group, my_x), quarters[group].at[my_x], line_load.at[i])
                  for i, group in enumerate(OWNERS)]
    own_copies.append(pltpu.make_async_copy(t_hbm, t_line.at[my_x], line_load.at[2]))
    swap_line = to_mate(line_part, line_other, line_send.at[4, 0], line_recv.at[4, 0])
    my_half = pl.ds(pl.multiple_of(me * (HALF // 2), 8), HALF // 2)
    their_half = pl.ds(pl.multiple_of(mate * (HALF // 2), 8), HALF // 2)
    give_half = to_mate(line_gram.at[:, my_half], line_gram.at[:, my_half], line_send.at[4, 1], line_recv.at[4, 1])
    take_half = to_mate(line_gram.at[:, my_half], line_gram.at[:, their_half], line_send.at[4, 1], line_recv.at[4, 1])

    def block_diagonal(t_rows, group):
        size = t_rows.shape[0]
        column = t_rows[:, group * WIDTH:(group + 1) * WIDTH]
        wide = jnp.concatenate([column] * (size // WIDTH), axis=1)
        row_id = lax.broadcasted_iota(jnp.int32, (size, size), 0)
        col_id = lax.broadcasted_iota(jnp.int32, (size, size), 1)
        return jnp.where(row_id // WIDTH == col_id // WIDTH, wide, 0.0), row_id, col_id

    def merged(t_rows, group, gram):
        t_mat, row_id, col_id = block_diagonal(t_rows, group)
        size = WIDTH
        while size < gram.shape[0]:
            pick = (row_id // size + 1 == col_id // size) & (row_id // (2 * size) == col_id // (2 * size))
            t_mat = t_mat - dot_nn(dot_nn(t_mat, jnp.where(pick, gram, 0.0)), t_mat)
            size *= 2
        return t_mat

    def line_1():
        for kind in range(3):
            for copy in line_copies(kind, True):
                copy.wait_recv()
        for copy in own_copies:
            copy.wait()
        for i, group in enumerate(OWNERS):
            rows = quarters[group][...].reshape(HALF, QUARTERS[group])
            line_part[i] = dot_nt(rows, rows)
        swap_line.start()

    def line_2():
        swap_line.wait_recv()
        line_half[my_x] = line_part[:, my_half] + line_other[:, my_half]
        for copy in line_copies(3, False):
            copy.start()

    def line_3():
        for copy in line_copies(3, True):
            copy.wait_recv()
        line_gram[:, my_half] = (line_half[0] + line_half[1]) + (line_half[2] + line_half[3])
        give_half.start()

    def line_4():
        take_half.wait_recv()
        mine = pl.ds(pl.multiple_of(my_x * WIDTH, 8), WIDTH)
        for i, group in enumerate(OWNERS):
            line_t[i] = merged(t_line[...].reshape(HALF, TILE), group, line_gram[i])
            buf_t[coords[0], coords[1], coords[2], i] = line_t[i, mine]

    actions = {'b': begin, 'f': forward, 'e': finish}
    lines = {'L1': line_1, 'L2': line_2, 'L3': line_3, 'L4': line_4}

    def act(events):
        for event in events.split():
            if event in lines:
                lines[event]()
            else:
                actions[event[0]](*(int(digit) for digit in event[1:]))

    load(2)
    for kind in range(3):
        for copy in line_copies(kind, False):
            copy.start()
    for copy in own_copies:
        copy.start()
    load(1)
    load(0)
    loaded(2)
    begin(2, 0)
    loaded(1)
    begin(1, 0)
    loaded(0)
    begin(0, 0)
    keep.start()
    give.start()
    for events in PRELUDE:
        act(events)
    keep.wait()
    take.wait_recv()

    def apply_group(group):
        buf = bufs[group]
        tiles = TILES[group]
        first_row = local_rows - tiles * TILE

        def block_step(step, carry):
            blk = 7 - step
            z, y = blk // 2, 2 * lax.rem(blk, 2)
            slot = lax.rem(step, 2)

            def run(where):
                for when, events in EVENTS.get((group, where), {}).items():
                    @pl.when(step == when)
                    def _():
                        act(events)

            def block_of(tile, count):
                pieces = [buf[z, pl.ds(y, 2), :, tile + i].reshape(BLOCK, TILE) for i in range(count)]
                return jnp.concatenate(pieces, axis=1)

            def rows_of(tile, count):
                return pl.ds(pl.multiple_of(first_row + tile * TILE, TILE), count * TILE)

            def over_rows(body):
                @pl.when(blk >= 4)
                def _():
                    body(4, 4)

                lax.fori_loop(blk // 4, tiles // 8, lambda c, carry: (body(8 * c, 8), carry)[1], 0)

            run('before')
            if group in OWNERS:
                w_part[slot] = jnp.zeros(w_part.shape[1:], jnp.float32)

                def products(tile, count):
                    v_c = block_of(tile, count)
                    x_c = x_buf[:, rows_of(tile, count)]
                    w_part[slot] += dot_nt(jnp.concatenate([x_c, v_c[:HALF]], axis=0), v_c)

                over_rows(products)
                swap = to_mate(w_part.at[slot], w_other.at[slot], swap_send.at[0, slot], swap_recv.at[0, slot])
                swap.start()
                run('mid')
                swap.wait()
                total = w_part[slot] + w_other[slot]
                w_t, cross = total[:cols], total[cols:, HALF:]
                i = OWNERS.index(group)
                t_1 = buf_t[z, y, :, i].reshape(HALF, HALF)
                t_2 = buf_t[z, y + 1, :, i].reshape(HALF, HALF)
            else:
                g_part[slot] = jnp.zeros(g_part.shape[1:], jnp.float32)

                def gram_products(tile, count):
                    v_c = block_of(tile, count)
                    g_part[slot] += dot_nt(v_c, v_c)

                over_rows(gram_products)
                g_swap = to_mate(g_part.at[slot], g_other.at[slot], swap_send.at[1, slot], swap_recv.at[1, slot])
                g_swap.start()
                w_rows = pl.ds(0, cols)
                w_part[slot, w_rows] = jnp.zeros((cols, BLOCK), jnp.float32)

                def w_products(tile, count):
                    w_part[slot, w_rows] += dot_nt(x_buf[:, rows_of(tile, count)], block_of(tile, count))

                over_rows(w_products)
                swap = to_mate(w_part.at[slot, w_rows], w_other.at[slot, w_rows], swap_send.at[0, slot], swap_recv.at[0, slot])
                swap.start()
                g_swap.wait()
                gram = g_part[slot] + g_other[slot]
                t_rows = buf[z, pl.ds(y, 2), :, tiles].reshape(BLOCK, TILE)
                t_1 = merged(t_rows[:HALF], group, gram[:HALF, :HALF])
                t_2 = merged(t_rows[HALF:], group, gram[HALF:, HALF:])
                cross = gram[:HALF, HALF:]
                run('mid')
                swap.wait()
                w_t = w_part[slot, w_rows] + w_other[slot, w_rows]

            y_2 = dot_nt(w_t[:, HALF:], t_2)
            y_1 = dot_nt(w_t[:, :HALF] - dot_nt(y_2, cross), t_1)
            y_t = jnp.concatenate([y_1, y_2], axis=1)

            def update(tile, count):
                x_buf[:, rows_of(tile, count)] -= dot_nn(y_t, block_of(tile, count))

            over_rows(update)
            return carry

        lax.fori_loop(0, 8, block_step, 0)

    apply_group(2)
    apply_group(1)
    apply_group(0)
    out_ref[...] = x_buf[...]

    give.wait_send()
    swap_line.wait_send()
    give_half.wait_send()
    for kind in range(4):
        for copy in line_copies(kind, False):
            copy.wait_send()
    for key in message_keys():
        for copy in messages(*key, False):
            copy.wait_send()


def solution(mesh):
    def local_apply(v_loc, t_loc, z_loc):
        groups, width = t_loc.shape[0], t_loc.shape[1]
        local_rows = v_loc.shape[0]
        cols = 2 * z_loc.shape[1]
        t_tile = jnp.pad(t_loc.transpose(1, 0, 2).reshape(width, groups * width), ((0, 0), (0, TILE - groups * width)))
        any_spec = pl.BlockSpec(memory_space=pl.ANY)
        dma = pltpu.SemaphoreType.DMA

        def vmem(*shape):
            return pltpu.VMEM(shape, jnp.float32)

        x_t = pl.pallas_call(
            kernel,
            out_shape=jax.ShapeDtypeStruct((cols, local_rows), jnp.float32),
            in_specs=[any_spec, any_spec, any_spec],
            out_specs=pl.BlockSpec(memory_space=pltpu.VMEM),
            scratch_shapes=[
                *(vmem(SIDE, SIDE, SIDE, TILES[group] + EXTRA[group], WIDTH, TILE) for group in (2, 1, 0)),
                vmem(SIDE, SIDE, SIDE, len(OWNERS), WIDTH, TILE),
                vmem(cols, local_rows),
                vmem(2, cols + HALF, BLOCK), vmem(2, cols + HALF, BLOCK),
                vmem(2, BLOCK, BLOCK), vmem(2, BLOCK, BLOCK),
                *(vmem(SIDE, WIDTH, QUARTERS[group]) for group in OWNERS), vmem(SIDE, WIDTH, TILE),
                vmem(2, HALF, HALF), vmem(2, HALF, HALF), vmem(SIDE, 2, HALF // 2, HALF),
                vmem(2, HALF, HALF), vmem(2, HALF, HALF),
                dma((3,)), dma((3,)), dma((len(TABLE),)), dma((len(TABLE),)), dma((2, 2)), dma((2, 2)),
                dma((5, 3)), dma((5, 3)), dma((3,)),
            ],
            compiler_params=pltpu.CompilerParams(collective_id=0, has_side_effects=True, vmem_limit_bytes=67043328),
        )(v_loc.T, t_tile, z_loc.T)
        return x_t.T

    return jax.shard_map(local_apply, mesh=mesh,
                         in_specs=(P('row', 'col'), P('col', None, None), P(None, ('col', 'row'))),
                         out_specs=P('row', 'col'), check_vma=False)
```

time: 288 us -> 246 us (0.85)
  Pallas kernels: 284 us -> 242 us
    pallas_call x1, Pallas kernels: 284 us -> 242 us  [local_apply(): pl.pallas_call(kernel, out_shape=jax.ShapeDtypeStruct((cols, local_rows),...]
where the time goes in v4:
time: 246 us
  Pallas kernels  242 us (98%)
  local copies, waits for them, and re-layouts  3.61 us (1%)
    pallas_call x1, Pallas kernels, local_apply(): pl.pallas_call(kernel, out_shape=jax.ShapeDtypeStruct((cols, local_rows),...  242 us

profile of v4, /device:TPU:1, one launch (start us, length us, event | category | flops | bytes accessed | tf_op | source)
XLA Modules:
  0.0 245.9 jit_solution(1259542818338910660)
XLA Ops:
  0.0 0.8 copy.5
  0.8 0.1 reshape.3
  0.9 0.6 pad.4.t_hbm
  1.5 242.3 %shard_map.37 = f32[64,3072]{1,0:T(8,128)} custom-call(f32[96,3072]{1,0:T(8,128)} %bitcast.5, f32[32,128]{1,0:T(8,128)} %pad.4.t_hbm, f32[32,6144]{1,0:T(8,128)} %bitcast.6), custom_call_target="tpu_custom_call" | custom-call | tf_op jit(solution)/shard_map/pallas_call | solution.py:420
  243.8 2.1 copy.7

commit v5 on v4

--- a/solution.py
+++ b/solution.py
@@ -30,12 +30,12 @@
     'b221 f223 e11 e30', 'b31 f222 f22 b220', 'f221 e223 b12 f31', 'b01 e222 f220 e22',
 )
 EVENTS = {
-    (2, 'before'): {3: 'e220', 5: 'f122', 6: 'e123', 7: 'f32'},
-    (2, 'mid'): {0: 'e221', 1: 'b123', 2: 'f12', 3: 'b122 f123', 4: 'e31', 5: 'b32 f01', 6: 'e122', 7: 'b121'},
+    (2, 'before'): {3: 'e220', 5: 'f122', 6: 'e123'},
+    (2, 'mid'): {0: 'e221', 1: 'e31 b32 b123', 2: 'f12', 3: 'b122 f123', 4: 'f32', 5: 'f01', 6: 'e122', 7: 'b121'},
     (1, 'before'): {0: 'e32 e12', 2: 'f120', 5: 'f02 f023'},
-    (1, 'mid'): {0: 'b120 f121', 1: 'e01 b02', 3: 'e121 b023', 4: 'e120', 5: 'b022', 6: 'e023', 7: 'f022'},
-    (0, 'before'): {0: 'b021 e022 b020 f021 e02', 4: 'e021', 6: 'e020'},
-    (0, 'mid'): {1: 'f020'},
+    (1, 'mid'): {0: 'b120 f121', 1: 'e01 b02', 3: 'e121 b023', 4: 'e120', 5: 'b022', 6: 'e023 b021', 7: 'f022'},
+    (0, 'before'): {0: 'e02', 2: 'e022', 4: 'e021', 6: 'e020'},
+    (0, 'mid'): {0: 'f021 b020', 2: 'f020'},
 }
 
 

time: 246 us -> 261 us (1.061)
  Pallas kernels: 242 us -> 257 us
    pallas_call x1, Pallas kernels: 242 us -> 257 us  [local_apply(): pl.pallas_call(kernel, out_shape=jax.ShapeDtypeStruct((cols, local_rows),...]
where the time goes in v5:
time: 261 us
  Pallas kernels  257 us (98%)
  local copies, waits for them, and re-layouts  3.61 us (1%)
    pallas_call x1, Pallas kernels, local_apply(): pl.pallas_call(kernel, out_shape=jax.ShapeDtypeStruct((cols, local_rows),...  257 us

profile of v5, /device:TPU:1, one launch (start us, length us, event | category | flops | bytes accessed | tf_op | source)
XLA Modules:
  0.0 260.7 jit_solution(16882034784822740061)
XLA Ops:
  0.0 0.8 copy.5
  0.8 0.1 reshape.3
  0.9 0.6 pad.4.t_hbm
  1.5 257.1 %shard_map.37 = f32[64,3072]{1,0:T(8,128)} custom-call(f32[96,3072]{1,0:T(8,128)} %bitcast.5, f32[32,128]{1,0:T(8,128)} %pad.4.t_hbm, f32[32,6144]{1,0:T(8,128)} %bitcast.6), custom_call_target="tpu_custom_call" | custom-call | tf_op jit(solution)/shard_map/pallas_call | solution.py:420
  258.7 2.1 copy.7

commit v6 on v5

--- a/solution.py
+++ b/solution.py
@@ -13,29 +13,29 @@
 SIDE = 4
 WIDTH = 32
 TILES = {2: 8, 1: 16, 0: 24}
-EXTRA = {2: 1, 1: 0, 0: 0}
 OWNERS = (1, 0)
-ROUND_T = 3
 QUARTERS = {group: TILES[group] // SIDE * TILE for group in OWNERS}
 ORDERS = ((2, 1, 0), (1, 0, 2), (0, 2, 1))
 RANGES = {
-    2: ((7, 9), (0, 3), (3, 7)),
-    1: ((12, 16), (0, 7), (7, 12)),
-    0: ((18, 24), (0, 10), (10, 18)),
-    3: ((0, 0), (0, 1), (1, 2)),
+    2: ((8, 9), (0, 5), (5, 8)),
+    1: ((14, 17), (0, 7), (7, 14)),
+    0: ((20, 25), (0, 12), (12, 20)),
 }
-ROUNDS = (2, 1, 0, ROUND_T)
 PRELUDE = (
-    'L1 f20 f10 L2', 'f00 e20 b21 e10', 'b11 L3 e00 L4', 'b30 f21 f11 f30', 'e21 b22 b223 b222',
-    'b221 f223 e11 e30', 'b31 f222 f22 b220', 'f221 e223 b12 f31', 'b01 e222 f220 e22',
+    'b200.b201.b202.r1.f200.f202.f201.e202.b212',
+    'e201.b211.e200.b210.m11.f212.m12.f210.f211',
+    'e210.e212.b2223.b220.r0.b2222.m13.m14.f2223',
+    'b100.b101.b102.e211.b2213.f2213.e2213.b2212.f2222',
+    'f220.b2211.f100.e2223.m01.f102.b2221.f2212.f101',
+    'm02.f2211.e2222.e220',
 )
 EVENTS = {
-    (2, 'before'): {3: 'e220', 5: 'f122', 6: 'e123'},
-    (2, 'mid'): {0: 'e221', 1: 'e31 b32 b123', 2: 'f12', 3: 'b122 f123', 4: 'f32', 5: 'f01', 6: 'e122', 7: 'b121'},
-    (1, 'before'): {0: 'e32 e12', 2: 'f120', 5: 'f02 f023'},
-    (1, 'mid'): {0: 'b120 f121', 1: 'e01 b02', 3: 'e121 b023', 4: 'e120', 5: 'b022', 6: 'e023 b021', 7: 'f022'},
-    (0, 'before'): {0: 'e02', 2: 'e022', 4: 'e021', 6: 'e020'},
-    (0, 'mid'): {0: 'f021 b020', 2: 'f020'},
+    (2, 'before'): {1: 'm03', 3: 'f111', 4: 'f001', 5: 'e112.e000.b1223.b010.e110.b120', 6: 'f1213.f1223.f1212.f120.b1222.b1210.f1211.f010.e2210', 7: 'b1221'},
+    (2, 'mid'): {0: 'e102.b112.b2220.e100.b110.f2221.e2212', 1: 'e101.b111.m04.e2211.b000.b001.b002.f2220', 2: 'f112.f110', 3: 'e2221.f000', 4: 'f002.b2210.e2220', 5: 'e111.e001.b1213.b1212.b1211.b011.f2210.e002', 6: 'e1213.e1223.e1212', 7: 'f1222.f011.f1210.b012'},
+    (1, 'before'): {0: 'e010.e1211.b1220.f1221.e1210.e120', 1: 'f012.b020', 2: 'e011', 3: 'e012', 4: 'f0213.e1221', 5: 'e1220', 6: 'f0223.f0212', 7: 'b0222'},
+    (1, 'mid'): {1: 'e1222', 2: 'f1220.b0213', 4: 'f020.b0223.b0212', 5: 'e0213', 7: 'b0211'},
+    (0, 'before'): {0: 'e0223.e0212.f0222.e020', 1: 'b0221', 4: 'e0221', 6: 'e0220'},
+    (0, 'mid'): {0: 'f0211', 1: 'e0222.b0210', 2: 'f0221.e0211', 3: 'f0210.b0220', 4: 'f0220', 5: 'e0210'},
 }
 
 
@@ -65,22 +65,17 @@
     return (*index, pl.ds(low, high - low)) if low < high else None
 
 
-def planes_of(group, phase):
-    return (None, 3, 2, 1, 0) if phase == 2 and group != ROUND_T else (None,)
-
-
-def parts_of(group, phase, plane):
-    if planes_of(group, phase) == (None,):
-        return (0, 1, 2)
-    return (0,) if plane is None else (1, 2)
+def planes_of(part, phase):
+    return (3, 2, 1, 0) if part and phase == 2 else (None,)
 
 
 def message_keys():
-    for group in ROUNDS:
+    for group in TILES:
         for phase in range(3):
-            for plane in planes_of(group, phase):
-                for piece in range(3):
-                    yield group, phase, plane, piece
+            for part in range(3):
+                for plane in planes_of(part, phase):
+                    for piece in range(3):
+                        yield group, phase, part, plane, piece
 
 
 def half_of(piece, way):
@@ -89,22 +84,21 @@
 
 def semaphore_table():
     table = {}
-    for group, phase, plane, piece in message_keys():
-        for part in parts_of(group, phase, plane):
-            for way in range(2):
-                if regions(group, part, phase, plane, (0, 0, 0), 0, half_of(piece, way)) is not None:
-                    table[group, phase, plane, piece, part, way] = len(table)
+    for group, phase, part, plane, piece in message_keys():
+        for way in range(2):
+            if regions(group, part, phase, plane, (0, 0, 0), 0, half_of(piece, way)) is not None:
+                table[group, phase, part, plane, piece, way] = len(table)
     return table
 
 
 TABLE = semaphore_table()
 
 
-def kernel(v_hbm, t_hbm, z_hbm, out_ref, buf2, buf1, buf0, buf_t, x_buf, w_part, w_other, g_part, g_other, quarters_1,
+def kernel(v_hbm, t_hbm, z_hbm, out_ref, buf2, buf1, buf0, x_buf, w_part, w_other, g_part, g_other, quarters_1,
            quarters_0, t_line,
            line_part, line_other, line_half, line_gram, line_t,
            load_sem, x_sem, send_sem, recv_sem, swap_send, swap_recv, line_send, line_recv, line_load):
-    bufs = {2: buf2, 1: buf1, 0: buf0, ROUND_T: buf_t}
+    bufs = {2: buf2, 1: buf1, 0: buf0}
     quarters = {1: quarters_1, 0: quarters_0}
     cols, local_rows = x_buf.shape
     share = cols // 2
@@ -158,37 +152,36 @@
     give = to_mate(z_hbm.at[:, theirs], my_cols, x_sem.at[1], x_sem.at[2])
     take = to_mate(z_hbm.at[:, theirs], their_cols, x_sem.at[1], x_sem.at[2])
 
-    def messages(group, phase, plane, piece, incoming):
+    def messages(group, phase, part, plane, piece, incoming):
         copies = []
-        for part in parts_of(group, phase, plane):
-            axis = ORDERS[part][phase]
-            for way in range(2):
-                sign = 1 - 2 * way
-                pos = shifted(axis, (-sign if piece == 2 else 0) + (-sign if incoming else 0))
-                index = regions(group, part, phase, plane, coords, pos, half_of(piece, way))
-                if index is None:
-                    continue
-                number = TABLE[group, phase, plane, piece, part, way]
-                ref = bufs[group].at[index]
-                copies.append(pltpu.make_async_remote_copy(
-                    src_ref=ref, dst_ref=ref, send_sem=send_sem.at[number], recv_sem=recv_sem.at[number],
-                    device_id=neighbour(axis, sign), device_id_type=MESH))
+        axis = ORDERS[part][phase]
+        for way in range(2):
+            sign = 1 - 2 * way
+            pos = shifted(axis, (-sign if piece == 2 else 0) + (-sign if incoming else 0))
+            index = regions(group, part, phase, plane, coords, pos, half_of(piece, way))
+            if index is None:
+                continue
+            number = TABLE[group, phase, part, plane, piece, way]
+            ref = bufs[group].at[index]
+            copies.append(pltpu.make_async_remote_copy(
+                src_ref=ref, dst_ref=ref, send_sem=send_sem.at[number], recv_sem=recv_sem.at[number],
+                device_id=neighbour(axis, sign), device_id_type=MESH))
         return copies
 
-    def begin(group, phase, plane=None):
+    def begin(group, phase, part, plane=None):
         for piece in range(2):
-            for copy in messages(group, phase, plane, piece, False):
+            for copy in messages(group, phase, part, plane, piece, False):
                 copy.start()
 
-    def forward(group, phase, plane=None):
-        for copy in messages(group, phase, plane, 0, True):
+    def forward(group, phase, part, plane=None):
+        for copy in messages(group, phase, part, plane, 0, True):
             copy.wait_recv()
-        for copy in messages(group, phase, plane, 2, False):
+        for copy in messages(group, phase, part, plane, 2, False):
             copy.start()
 
-    def finish(group, phase, plane=None):
+    def finish(group, phase, part, plane=None):
         for piece in range(1, 3):
-            for copy in messages(group, phase, plane, piece, True):
+            for copy in messages(group, phase, part, plane, piece, True):
                 copy.wait_recv()
 
     def quarter(group, x):
@@ -196,30 +189,32 @@
         lanes = pl.ds(pl.multiple_of(first + x * QUARTERS[group], TILE), QUARTERS[group])
         return v_hbm.at[pl.ds(group * WIDTH, WIDTH), lanes]
 
-    def line_copies(kind, incoming):
+    def line_copies(kind, i, incoming):
         copies = []
         for by in range(1, SIDE):
-            other = shifted(2, by)
             slot = shifted(2, -by) if incoming else my_x
-            if kind < 2:
-                src, dst = quarter(OWNERS[kind], other), quarters[OWNERS[kind]].at[slot]
-            elif kind == 2:
+            if kind == 0:
+                src, dst = quarter(OWNERS[i], shifted(2, by)), quarters[OWNERS[i]].at[slot]
+            elif kind == 1:
+                src, dst = line_half.at[i, my_x], line_half.at[i, slot]
+            else:
                 src, dst = t_hbm, t_line.at[slot]
-            else:
-                src, dst = line_half.at[my_x], line_half.at[slot]
             copies.append(pltpu.make_async_remote_copy(
-                src_ref=src, dst_ref=dst, send_sem=line_send.at[kind, by - 1], recv_sem=line_recv.at[kind, by - 1],
+                src_ref=src, dst_ref=dst, send_sem=line_send.at[i, kind, by - 1], recv_sem=line_recv.at[i, kind, by - 1],
                 device_id=neighbour(2, by), device_id_type=MESH))
         return copies
 
-    own_copies = [pltpu.make_async_copy(quarter(group, my_x), quarters[group].at[my_x], line_load.at[i])
-                  for i, group in enumerate(OWNERS)]
-    own_copies.append(pltpu.make_async_copy(t_hbm, t_line.at[my_x], line_load.at[2]))
-    swap_line = to_mate(line_part, line_other, line_send.at[4, 0], line_recv.at[4, 0])
+    own_quarters = [pltpu.make_async_copy(quarter(group, my_x), quarters[group].at[my_x], line_load.at[i])
+                    for i, group in enumerate(OWNERS)]
+    own_t = pltpu.make_async_copy(t_hbm, t_line.at[my_x], line_load.at[2])
     my_half = pl.ds(pl.multiple_of(me * (HALF // 2), 8), HALF // 2)
     their_half = pl.ds(pl.multiple_of(mate * (HALF // 2), 8), HALF // 2)
-    give_half = to_mate(line_gram.at[:, my_half], line_gram.at[:, my_half], line_send.at[4, 1], line_recv.at[4, 1])
-    take_half = to_mate(line_gram.at[:, my_half], line_gram.at[:, their_half], line_send.at[4, 1], line_recv.at[4, 1])
+
+    def swap_line(i):
+        return to_mate(line_part.at[i], line_other.at[i], line_send.at[i, 3, 0], line_recv.at[i, 3, 0])
+
+    def swap_half(i, half):
+        return to_mate(line_gram.at[i, my_half], line_gram.at[i, half], line_send.at[i, 3, 1], line_recv.at[i, 3, 1])
 
     def block_diagonal(t_rows, group):
         size = t_rows.shape[0]
@@ -238,62 +233,57 @@
             size *= 2
         return t_mat
 
-    def line_1():
-        for kind in range(3):
-            for copy in line_copies(kind, True):
+    def trade(group):
+        i = OWNERS.index(group)
+        own_quarters[i].start()
+        for copy in line_copies(0, i, False):
+            copy.start()
+        if i == 0:
+            own_t.start()
+            for copy in line_copies(2, i, False):
+                copy.start()
+
+    def merge(group, stage):
+        i = OWNERS.index(group)
+        if stage == 1:
+            for copy in line_copies(0, i, True):
                 copy.wait_recv()
-        for copy in own_copies:
-            copy.wait()
-        for i, group in enumerate(OWNERS):
+            own_quarters[i].wait()
             rows = quarters[group][...].reshape(HALF, QUARTERS[group])
             line_part[i] = dot_nt(rows, rows)
-        swap_line.start()
-
-    def line_2():
-        swap_line.wait_recv()
-        line_half[my_x] = line_part[:, my_half] + line_other[:, my_half]
-        for copy in line_copies(3, False):
-            copy.start()
-
-    def line_3():
-        for copy in line_copies(3, True):
-            copy.wait_recv()
-        line_gram[:, my_half] = (line_half[0] + line_half[1]) + (line_half[2] + line_half[3])
-        give_half.start()
-
-    def line_4():
-        take_half.wait_recv()
-        mine = pl.ds(pl.multiple_of(my_x * WIDTH, 8), WIDTH)
-        for i, group in enumerate(OWNERS):
+            swap_line(i).start()
+        elif stage == 2:
+            swap_line(i).wait_recv()
+            line_half[i, my_x] = line_part[i, my_half] + line_other[i, my_half]
+            for copy in line_copies(1, i, False):
+                copy.start()
+        elif stage == 3:
+            for copy in line_copies(1, i, True):
+                copy.wait_recv()
+            line_gram[i, my_half] = (line_half[i, 0] + line_half[i, 1]) + (line_half[i, 2] + line_half[i, 3])
+            swap_half(i, my_half).start()
+        else:
+            swap_half(i, their_half).wait_recv()
+            if i == 0:
+                own_t.wait()
+                for copy in line_copies(2, i, True):
+                    copy.wait_recv()
             line_t[i] = merged(t_line[...].reshape(HALF, TILE), group, line_gram[i])
-            buf_t[coords[0], coords[1], coords[2], i] = line_t[i, mine]
-
-    actions = {'b': begin, 'f': forward, 'e': finish}
-    lines = {'L1': line_1, 'L2': line_2, 'L3': line_3, 'L4': line_4}
+            mine = pl.ds(pl.multiple_of(my_x * WIDTH, 8), WIDTH)
+            bufs[group][coords[0], coords[1], coords[2], TILES[group]] = line_t[i, mine]
+
+    actions = {'b': begin, 'f': forward, 'e': finish, 'r': trade, 'm': merge}
 
     def act(events):
-        for event in events.split():
-            if event in lines:
-                lines[event]()
-            else:
-                actions[event[0]](*(int(digit) for digit in event[1:]))
-
-    load(2)
-    for kind in range(3):
-        for copy in line_copies(kind, False):
-            copy.start()
-    for copy in own_copies:
-        copy.start()
-    load(1)
-    load(0)
-    loaded(2)
-    begin(2, 0)
-    loaded(1)
-    begin(1, 0)
-    loaded(0)
-    begin(0, 0)
+        for event in events.split('.'):
+            actions[event[0]](*(int(digit) for digit in event[1:]))
+
+    for group in TILES:
+        load(group)
     keep.start()
     give.start()
+    for group in TILES:
+        loaded(group)
     for events in PRELUDE:
         act(events)
     keep.wait()
@@ -345,9 +335,8 @@
                 swap.wait()
                 total = w_part[slot] + w_other[slot]
                 w_t, cross = total[:cols], total[cols:, HALF:]
-                i = OWNERS.index(group)
-                t_1 = buf_t[z, y, :, i].reshape(HALF, HALF)
-                t_2 = buf_t[z, y + 1, :, i].reshape(HALF, HALF)
+                t_1 = buf[z, y, :, tiles].reshape(HALF, HALF)
+                t_2 = buf[z, y + 1, :, tiles].reshape(HALF, HALF)
             else:
                 g_part[slot] = jnp.zeros(g_part.shape[1:], jnp.float32)
 
@@ -395,11 +384,12 @@
     out_ref[...] = x_buf[...]
 
     give.wait_send()
-    swap_line.wait_send()
-    give_half.wait_send()
-    for kind in range(4):
-        for copy in line_copies(kind, False):
-            copy.wait_send()
+    for i in range(len(OWNERS)):
+        swap_line(i).wait_send()
+        swap_half(i, my_half).wait_send()
+        for kind in range(3 if i == 0 else 2):
+            for copy in line_copies(kind, i, False):
+                copy.wait_send()
     for key in message_keys():
         for copy in messages(*key, False):
             copy.wait_send()
@@ -423,16 +413,15 @@
             in_specs=[any_spec, any_spec, any_spec],
             out_specs=pl.BlockSpec(memory_space=pltpu.VMEM),
             scratch_shapes=[
-                *(vmem(SIDE, SIDE, SIDE, TILES[group] + EXTRA[group], WIDTH, TILE) for group in (2, 1, 0)),
-                vmem(SIDE, SIDE, SIDE, len(OWNERS), WIDTH, TILE),
+                *(vmem(SIDE, SIDE, SIDE, TILES[group] + 1, WIDTH, TILE) for group in (2, 1, 0)),
                 vmem(cols, local_rows),
                 vmem(2, cols + HALF, BLOCK), vmem(2, cols + HALF, BLOCK),
                 vmem(2, BLOCK, BLOCK), vmem(2, BLOCK, BLOCK),
                 *(vmem(SIDE, WIDTH, QUARTERS[group]) for group in OWNERS), vmem(SIDE, WIDTH, TILE),
-                vmem(2, HALF, HALF), vmem(2, HALF, HALF), vmem(SIDE, 2, HALF // 2, HALF),
+                vmem(2, HALF, HALF), vmem(2, HALF, HALF), vmem(2, SIDE, HALF // 2, HALF),
                 vmem(2, HALF, HALF), vmem(2, HALF, HALF),
                 dma((3,)), dma((3,)), dma((len(TABLE),)), dma((len(TABLE),)), dma((2, 2)), dma((2, 2)),
-                dma((5, 3)), dma((5, 3)), dma((3,)),
+                dma((2, 4, 3)), dma((2, 4, 3)), dma((3,)),
             ],
             compiler_params=pltpu.CompilerParams(collective_id=0, has_side_effects=True, vmem_limit_bytes=67043328),
         )(v_loc.T, t_tile, z_loc.T)

time: 261 us -> 237 us (0.908)
  Pallas kernels: 257 us -> 233 us
    pallas_call x1, Pallas kernels: 257 us -> 233 us  [local_apply(): pl.pallas_call(kernel, out_shape=jax.ShapeDtypeStruct((cols, local_rows),...]
where the time goes in v6:
time: 237 us
  Pallas kernels  233 us (98%)
  local copies, waits for them, and re-layouts  3.61 us (2%)
    pallas_call x1, Pallas kernels, local_apply(): pl.pallas_call(kernel, out_shape=jax.ShapeDtypeStruct((cols, local_rows),...  233 us

profile of v6, /device:TPU:1, one launch (start us, length us, event | category | flops | bytes accessed | tf_op | source)
XLA Modules:
  0.0 236.7 jit_solution(17482730582409505690)
XLA Ops:
  0.0 0.8 copy.5
  0.8 0.1 reshape.3
  0.9 0.6 pad.4.t_hbm
  1.5 233.1 %shard_map.37 = f32[64,3072]{1,0:T(8,128)} custom-call(f32[96,3072]{1,0:T(8,128)} %bitcast.5, f32[32,128]{1,0:T(8,128)} %pad.4.t_hbm, f32[32,6144]{1,0:T(8,128)} %bitcast.6), custom_call_target="tpu_custom_call" | custom-call | tf_op jit(solution)/shard_map/pallas_call | solution.py:410
  234.7 2.1 copy.7

commit v7 on v6

--- a/solution.py
+++ b/solution.py
@@ -17,25 +17,26 @@
 QUARTERS = {group: TILES[group] // SIDE * TILE for group in OWNERS}
 ORDERS = ((2, 1, 0), (1, 0, 2), (0, 2, 1))
 RANGES = {
-    2: ((8, 9), (0, 5), (5, 8)),
-    1: ((14, 17), (0, 7), (7, 14)),
-    0: ((20, 25), (0, 12), (12, 20)),
+    2: ((7, 9), (0, 5), (5, 7)),
+    1: ((14, 17), (0, 9), (9, 14)),
+    0: ((21, 25), (0, 11), (11, 21)),
 }
 PRELUDE = (
-    'b200.b201.b202.r1.f200.f202.f201.e202.b212',
-    'e201.b211.e200.b210.m11.f212.m12.f210.f211',
-    'e210.e212.b2223.b220.r0.b2222.m13.m14.f2223',
-    'b100.b101.b102.e211.b2213.f2213.e2213.b2212.f2222',
-    'f220.b2211.f100.e2223.m01.f102.b2221.f2212.f101',
-    'm02.f2211.e2222.e220',
+    'b201.b200.b202.r1.f200.f202.f201.e202.b212',
+    'r0.e201.b211.e200.b210.m11.f212.m12.f210',
+    'f211.e210.b220.e211.b2213.f2213.e2213.b2212.b2211',
+    'm01.e212.b2223.b2222.m02.m13.f2212.b2221.m14',
+    'f2223.b101.b100.b102.f2211.f220.f2222.b2210.m03',
+    'e2212.f2221.f100.m04.b000.b002.e2223.e2211.f102',
+    'b2220.f101.f2210.e2222.e2221.f2220.e100.b110.e220',
 )
 EVENTS = {
-    (2, 'before'): {1: 'm03', 3: 'f111', 4: 'f001', 5: 'e112.e000.b1223.b010.e110.b120', 6: 'f1213.f1223.f1212.f120.b1222.b1210.f1211.f010.e2210', 7: 'b1221'},
-    (2, 'mid'): {0: 'e102.b112.b2220.e100.b110.f2221.e2212', 1: 'e101.b111.m04.e2211.b000.b001.b002.f2220', 2: 'f112.f110', 3: 'e2221.f000', 4: 'f002.b2210.e2220', 5: 'e111.e001.b1213.b1212.b1211.b011.f2210.e002', 6: 'e1213.e1223.e1212', 7: 'f1222.f011.f1210.b012'},
-    (1, 'before'): {0: 'e010.e1211.b1220.f1221.e1210.e120', 1: 'f012.b020', 2: 'e011', 3: 'e012', 4: 'f0213.e1221', 5: 'e1220', 6: 'f0223.f0212', 7: 'b0222'},
-    (1, 'mid'): {1: 'e1222', 2: 'f1220.b0213', 4: 'f020.b0223.b0212', 5: 'e0213', 7: 'b0211'},
-    (0, 'before'): {0: 'e0223.e0212.f0222.e020', 1: 'b0221', 4: 'e0221', 6: 'e0220'},
-    (0, 'mid'): {0: 'f0211', 1: 'e0222.b0210', 2: 'f0221.e0211', 3: 'f0210.b0220', 4: 'f0220', 5: 'e0210'},
+    (2, 'before'): {1: 'e102.b112.e2210.e2220', 4: 'e112.b1223', 6: 'b1213', 7: 'f1222'},
+    (2, 'mid'): {0: 'f000.f002.e101.b111', 1: 'e000.b010.e002.f110', 2: 'f112.b012.f010.f111.b001', 3: 'e110.b120', 4: 'f001.e010.b1222', 5: 'e111.f1223.f012', 6: 'e001.b1212.b1221.f120', 7: 'b1211.e012'},
+    (1, 'before'): {0: ('f1213.e1223.b1220.b011.f1212.f1221.e120', 'b1210.e1222.f1211.f1220.f011.e1213'), 1: 'e1212.e1221', 2: 'f1210.b020', 3: 'e011.f0223', 4: 'e1211', 5: 'e1210.f020', 6: 'b0212'},
+    (1, 'mid'): {0: 'b0223', 1: 'e1220', 4: 'b0213.b0222', 5: 'f0213.e0223', 6: 'f0222.e0213', 7: 'f0212'},
+    (0, 'before'): {0: 'b0211.b0221.e020', 3: 'e0211', 4: 'f0210', 6: 'e0210.e0220'},
+    (0, 'mid'): {0: 'e0212.e0222', 1: 'f0211.f0221', 2: 'b0210.b0220', 3: 'e0221', 4: 'f0220'},
 }
 
 
@@ -61,7 +62,7 @@
         index[order[1 if plane is not None and order[0] == 0 else 0]] = pl.ds(2 * half, 2)
     if plane is not None:
         index[0] = plane
-        low = max(low, 2 * plane)
+        low = max(low, 2 * plane + (half if part == 1 else 0))
     return (*index, pl.ds(low, high - low)) if low < high else None
 
 
@@ -120,15 +121,9 @@
                                             device_id={'row': mate}, device_id_type=MESH)
 
     for group in TILES:
-        for z in range(1, SIDE):
-            shape = (SIDE, SIDE, 2 * z, WIDTH, TILE)
-            bufs[group][z, :, :, 0:2 * z, :, :] = jnp.zeros(shape, jnp.float32)
-
-    barrier = pltpu.get_barrier_semaphore()
-    pl.semaphore_signal(barrier, inc=1, device_id={'row': mate}, device_id_type=MESH)
-    for axis, by in ((0, 1), (0, -1), (1, 1), (1, -1), (2, 1), (2, 2), (2, 3)):
-        pl.semaphore_signal(barrier, inc=1, device_id=neighbour(axis, by), device_id_type=MESH)
-    pl.semaphore_wait(barrier, 8)
+        for blk in range(1, 2 * SIDE):
+            z, y = blk // 2, 2 * (blk % 2)
+            bufs[group][z, y:y + 2, :, 0:blk, :, :] = jnp.zeros((2, SIDE, blk, WIDTH, TILE), jnp.float32)
 
     own = {group: bufs[group].at[coords[0], coords[1], coords[2]] for group in TILES}
 
@@ -143,6 +138,15 @@
     def loaded(group):
         tiles = pl.ds(0, TILES[group] + (1 if group == 2 else 0))
         pltpu.make_async_copy(own[group].at[tiles], own[group].at[tiles], load_sem.at[group]).wait()
+
+    for group in TILES:
+        load(group)
+
+    barrier = pltpu.get_barrier_semaphore()
+    pl.semaphore_signal(barrier, inc=1, device_id={'row': mate}, device_id_type=MESH)
+    for axis, by in ((0, 1), (0, -1), (1, 1), (1, -1), (2, 1), (2, 2), (2, 3)):
+        pl.semaphore_signal(barrier, inc=1, device_id=neighbour(axis, by), device_id_type=MESH)
+    pl.semaphore_wait(barrier, 8)
 
     mine = pl.ds(pl.multiple_of(me * local_rows, TILE), local_rows)
     theirs = pl.ds(pl.multiple_of(mate * local_rows, TILE), local_rows)
@@ -278,8 +282,6 @@
         for event in events.split('.'):
             actions[event[0]](*(int(digit) for digit in event[1:]))
 
-    for group in TILES:
-        load(group)
     keep.start()
     give.start()
     for group in TILES:
@@ -303,7 +305,8 @@
                 for when, events in EVENTS.get((group, where), {}).items():
                     @pl.when(step == when)
                     def _():
-                        act(events)
+                        for some in events if isinstance(events, tuple) else (events,):
+                            act(some)
 
             def block_of(tile, count):
                 pieces = [buf[z, pl.ds(y, 2), :, tile + i].reshape(BLOCK, TILE) for i in range(count)]

time: 237 us -> 229 us (0.966)
  Pallas kernels: 233 us -> 225 us
    pallas_call x1, Pallas kernels: 233 us -> 225 us  [local_apply(): pl.pallas_call(kernel, out_shape=jax.ShapeDtypeStruct((cols, local_rows),...]
where the time goes in v7:
time: 229 us
  Pallas kernels  225 us (98%)
  local copies, waits for them, and re-layouts  3.61 us (2%)
    pallas_call x1, Pallas kernels, local_apply(): pl.pallas_call(kernel, out_shape=jax.ShapeDtypeStruct((cols, local_rows),...  225 us

profile of v7, /device:TPU:1, one launch (start us, length us, event | category | flops | bytes accessed | tf_op | source)
XLA Modules:
  0.0 228.5 jit_solution(14428106932190661643)
XLA Ops:
  0.0 0.8 copy.5
  0.8 0.1 reshape.3
  0.9 0.6 pad.4.t_hbm
  1.5 224.9 %shard_map.37 = f32[64,3072]{1,0:T(8,128)} custom-call(f32[96,3072]{1,0:T(8,128)} %bitcast.5, f32[32,128]{1,0:T(8,128)} %pad.4.t_hbm, f32[32,6144]{1,0:T(8,128)} %bitcast.6), custom_call_target="tpu_custom_call" | custom-call | tf_op jit(solution)/shard_map/pallas_call | solution.py:413
  226.4 2.1 copy.7
